TPU v7x, 256 devices: a whole 4x4x8 slice. The times are simulated.
256 devices in a mesh: img: 16 (over z, core), pix: 16 (over x, y).
Axes of the slice: x: 4, y: 4, z: 8, core: 2. Of those that a mesh axis runs over, the one named last changes fastest.
Arguments:
- images: bfloat16 [51200, 16384], P('img', 'pix'), may hold values from -6 to 6
- classes: int32 [51200], P('img'), may hold values from 0 to 63
- ctf_table: bfloat16 [64, 16384], P(None, 'pix'), may hold values from -1 to 1, as said below
- weights: float32 [51200], P('img'), may hold values from 0.1 to 1
- probes: float32 [16384, 256], P('pix'), may hold values from -6 to 6
Outputs:
- basis: float32 [16384, 256], P('pix')
- factor: float32 [256, 256], replicated
Inputs may be any that keep to these rules, and one draw needn't show every extreme that they name: `ctf_table`: a smooth envelope over the pixel index times an independent magnitude and sign for each entry.
All inputs are finite; a program needn't handle non-finite values.
Results may differ from a plain program's by a relative error of at most 0.012.
Values may be sent and summed in bfloat16 or wider, within the bound.
A program may use at most 64 MiB of HBM per device.

v0:
```python
import jax
import jax.numpy as jnp
from jax import lax
from jax.sharding import Mesh
from jax.sharding import PartitionSpec as P

ITERS = 2
IMG = ("img_0", "img_1")


def cut_along(x, dim, devices):
    before, after = (x.shape[:dim], x.shape[dim + 1 :])
    return jnp.moveaxis(x.reshape(*before, devices, -1, *after), dim, 0)


def summed_on_arrival(x, axis, dim):
    blocks = cut_along(x, dim, lax.axis_size(axis))
    arrived = lax.all_to_all(blocks, axis, split_axis=0, concat_axis=0, tiled=True)
    return arrived.astype(jnp.float32).sum(axis=0)


def sent_to_all(x, axis):
    devices = lax.axis_size(axis)
    return lax.all_to_all(jnp.broadcast_to(x[None], (devices, *x.shape)), axis, 0, 0, tiled=True)


def joined_along(blocks, dim):
    lengths = list(blocks.shape[1:])
    lengths[dim] *= blocks.shape[0]
    return jnp.moveaxis(blocks, 0, dim).reshape(lengths)


def collect(x, axis, dim):
    blocks = sent_to_all(x, axis)
    return joined_along(blocks, dim)


def sum_in_two_steps(x, axes, dim):
    far, near = axes
    own = summed_on_arrival(cut_along(x, dim, lax.axis_size(far)), near, dim + 1)
    return jnp.sum(
        lax.all_to_all(own.astype(jnp.bfloat16), far, 0, 0, tiled=True).astype(jnp.float32), axis=0
    )


def rows_for(lines, devices):
    spare = -lines.shape[0] % devices
    if not spare:
        return lines
    return jnp.concatenate([lines, jnp.zeros((spare, *lines.shape[1:]), lines.dtype)])


def gather_axes(x, axes, dim):
    far, near = axes
    blocks = sent_to_all(sent_to_all(x, far), near)
    return joined_along(blocks.swapaxes(0, 1).reshape(-1, *x.shape), dim)


def sum_by_parts(x, axes):
    lines = x.reshape(-1, x.shape[-1])
    own = sum_in_two_steps(
        rows_for(lines, lax.axis_size(axes[0]) * lax.axis_size(axes[1])), axes, 0
    )
    whole = gather_axes(own.astype(jnp.bfloat16), axes, 0)
    return whole[: len(lines)].reshape(x.shape).astype(jnp.float32)


def summed_on_arrival_2(x, axis, dim):
    devices = lax.axis_size(axis)
    blocks = lax.all_to_all(cut_along(x, dim, devices), axis, 0, 0, tiled=True)
    return jnp.sum(blocks, axis=0)


def sum_by_parts_2(x, axes):
    lines = x.reshape(-1, x.shape[-1])
    padded = rows_for(lines, lax.axis_size(axes))
    whole = collect(summed_on_arrival_2(padded, axes, 0), axes, 0)
    return lax.slice_in_dim(whole, 0, len(lines)).reshape(x.shape)


def per_device(images, classes, ctf_table, weights, probes):
    onehot = (classes[:, None] == jnp.arange(ctf_table.shape[0])[None, :]).astype(jnp.bfloat16)
    filters = jnp.dot(onehot, ctf_table, preferred_element_type=jnp.float32)
    filtered = (images.astype(jnp.float32) * filters).astype(jnp.bfloat16)
    current = probes
    factor = jnp.zeros((probes.shape[1], probes.shape[1]), jnp.float32)
    for sweep in range(ITERS):
        probe_half = current.astype(jnp.bfloat16)
        share_rows = filtered.shape[0] // lax.axis_size("pix")
        shares = summed_on_arrival(
            jnp.dot(filtered, probe_half, preferred_element_type=jnp.float32).astype(jnp.bfloat16),
            "pix",
            0,
        )
        weight_share = lax.dynamic_slice_in_dim(
            weights, lax.axis_index("pix") * share_rows, share_rows, 0
        )
        scaled_share = (weight_share[:, None] * shares).astype(jnp.bfloat16)
        scaled = collect(scaled_share, "pix", 0)
        partial_sum = lax.dot_general(
            filtered, scaled, (((0,), (0,)), ((), ())), preferred_element_type=jnp.float32
        )
        image_sum = sum_by_parts(partial_sum.astype(jnp.bfloat16), ("img_0", "img_1"))
        gram_matrix = sum_by_parts_2(
            jnp.dot(image_sum.T, image_sum, precision=lax.Precision.HIGHEST), "pix"
        )
        factor = jnp.linalg.cholesky(gram_matrix)
        current = jax.scipy.linalg.solve_triangular(factor, image_sum.T, lower=True).T
    return (current, factor)


def solution(mesh):
    split = Mesh(mesh.devices.reshape(8, 2, mesh.shape["pix"]), ("img_0", "img_1", "pix"))
    return jax.shard_map(
        per_device,
        mesh=split,
        in_specs=(P(IMG, "pix"), P(IMG), P(None, "pix"), P(IMG), P("pix", None)),
        out_specs=(P("pix", None), P()),
        check_vma=False,
    )
```

profile of v0, /device:TPU:1, one launch (start us, length us, event | category | flops | bytes accessed | tf_op | source)
XLA Modules:
  0.0 384.9 jit_solution(7734217287325856505)
XLA Ops:
  1.5 4.3 %multiply_convert_fusion = bf16[3200,1024]{1,0:T(8,128)(2,1)S(1)} fusion(bf16[3200,1024]{1,0:T(8,128)(2,1)} %param.8, bf16[64,1024]{1,0:T(8,128)(2,1)S(1)} %copy-done, s32[3200]{0:T(1024)} %param.9), kind=kOutput, calls=%fused_computation.4 | convolution fusion | flops 429465600 | bytes 13251072 | tf_op jit(solution)/shard_map/dot_general | solution.py:83
  9.1 7.6 %all-to-all-start = ((bf16[16,200,256]{2,1,0:T(8,128)(2,1)}), bf16[16,200,256]{2,1,0:T(8,128)(2,1)S(1)}, u32[]{:S(2)}, u32[]{:S(2)}) async-start(bf16[16,200,256]{2,1,0:T(8,128)(2,1)} %bitcast), calls=%async_computation | async-start | bytes 3276800 | tf_op jit(solution)/shard_map/all_to_all | solution.py:18
  17.4 20.6 %all-to-all-done = bf16[16,200,256]{2,1,0:T(8,128)(2,1)S(1)} async-done(((bf16[16,200,256]{2,1,0:T(8,128)(2,1)}), bf16[16,200,256]{2,1,0:T(8,128)(2,1)S(1)}, u32[]{:S(2)}, u32[]{:S(2)}) %all-to-all-start) | async-done | bytes 1638432 | tf_op jit(solution)/shard_map/all_to_all | solution.py:18
  38.5 26.2 %all_to_all.80 = bf16[16,200,256]{2,1,0:T(8,128)(2,1)S(1)} all-to-all(bf16[16,200,256]{2,1,0:T(8,128)(2,1)S(1)} %broadcast_in_dim.16), channel_id=1, replica_groups=mesh['img_0'=8,'img_1'=2,'pix'=16] {'pix'}, dimensions={0} | all-to-all | bytes 3276800 | tf_op jit(solution)/shard_map/all_to_all | solution.py:24
  66.7 7.5 %all_to_all.81 = bf16[2,8,64,256]{3,2,1,0:T(8,128)(2,1)S(1)} all-to-all(bf16[2,8,64,256]{3,2,1,0:T(8,128)(2,1)S(1)} %bitcast.119), channel_id=1, replica_groups=mesh['img_0'=8,'img_1'=2,'pix'=16] {'img_1'}, dimensions={0} | all-to-all | bytes 1048576 | tf_op jit(solution)/shard_map/all_to_all | solution.py:18
  74.2 19.1 %all_to_all.82 = bf16[8,64,256]{2,1,0:T(8,128)(2,1)S(1)} all-to-all(bf16[8,64,256]{2,1,0:T(8,128)(2,1)S(1)} %reduce_sum.85), channel_id=1, replica_groups=mesh['img_0'=8,'img_1'=2,'pix'=16] {'img_0'}, dimensions={0} | all-to-all | bytes 524288 | tf_op jit(solution)/shard_map/all_to_all | solution.py:42
  93.4 12.2 %all_to_all.83 = bf16[8,64,256]{2,1,0:T(8,128)(2,1)S(1)} all-to-all(bf16[8,64,256]{2,1,0:T(8,128)(2,1)S(1)} %broadcast_in_dim.17), channel_id=1, replica_groups=mesh['img_0'=8,'img_1'=2,'pix'=16] {'img_0'}, dimensions={0} | all-to-all | bytes 524288 | tf_op jit(solution)/shard_map/all_to_all | solution.py:24
  105.6 6.8 %all_to_all.84 = bf16[2,8,64,256]{3,2,1,0:T(8,128)(2,1)S(1)} all-to-all(bf16[2,8,64,256]{3,2,1,0:T(8,128)(2,1)S(1)} %broadcast_in_dim.18), channel_id=1, replica_groups=mesh['img_0'=8,'img_1'=2,'pix'=16] {'img_1'}, dimensions={0} | all-to-all | bytes 1048576 | tf_op jit(solution)/shard_map/all_to_all | solution.py:24
  113.7 3.5 all-to-all-start.6
  117.3 7.7 %all-to-all-done.6 = f32[16,16,256]{2,1,0:T(8,128)S(1)} async-done(((f32[16,16,256]{2,1,0:T(8,128)}), f32[16,16,256]{2,1,0:T(8,128)S(1)}, u32[]{:S(2)}, u32[]{:S(2)}) %all-to-all-start.6) | async-done | bytes 262176 | tf_op jit(solution)/shard_map/all_to_all | solution.py:70
  125.7 4.0 %all-to-all-start.7 = ((f32[16,16,256]{2,1,0:T(8,128)}), f32[16,16,256]{2,1,0:T(8,128)S(1)}, u32[]{:S(2)}, u32[]{:S(2)}) async-start(f32[16,16,256]{2,1,0:T(8,128)} %broadcast_in_dim.19), calls=%async_computation.7 | async-start | bytes 524288 | tf_op jit(solution)/shard_map/all_to_all | solution.py:24
  129.9 7.2 %all-to-all-done.7 = f32[16,16,256]{2,1,0:T(8,128)S(1)} async-done(((f32[16,16,256]{2,1,0:T(8,128)}), f32[16,16,256]{2,1,0:T(8,128)S(1)}, u32[]{:S(2)}, u32[]{:S(2)}) %all-to-all-start.7) | async-done | bytes 262176 | tf_op jit(solution)/shard_map/all_to_all | solution.py:24
  137.2 11.7 %cholesky.130 = f32[128,128]{1,0:T(8,128)S(1)} custom-call(f32[128,128]{1,0:T(8,128)S(1)} %cholesky.194), custom_call_target="Cholesky" | custom-call | tf_op jit(solution)/shard_map/jit(cholesky)/cholesky | solution.py:107
  149.0 9.8 %custom-call.13 = f32[1,128,128]{1,2,0:T(8,128)S(1)} custom-call(f32[1,128,128]{2,1,0:T(8,128)S(1)} %get-tuple-element.57), custom_call_target="InvertDiagBlocksLowerTriangular" | custom-call | tf_op jit(solution)/shard_map/jit(cholesky)/cholesky | solution.py:107
  159.3 11.7 %cholesky.147 = f32[128,128]{1,0:T(8,128)S(1)} custom-call(f32[128,128]{1,0:T(8,128)S(1)} %convolution_subtract_fusion.3), custom_call_target="Cholesky" | custom-call | tf_op jit(solution)/shard_map/jit(cholesky)/cholesky | solution.py:107
  173.2 3.9 %while.4 = (s32[]{:T(128)}, f32[256,256]{1,0:T(8,128)S(1)}, s32[2,2]{1,0:T(2,128)S(1)}, f32[2,128,128]{2,1,0:T(8,128)S(1)}, s32[]{:T(128)}) while((s32[]{:T(128)}, f32[256,256]{1,0:T(8,128)S(1)}, s32[2,2]{1,0:T(2,128)S(1)}, f32[2,128,128]{2,1,0:T(8,128)S(1)}, s32[]{:T(128)}) %tuple.52), condition=%wide.while_cond, body=%wide.while_body.sunk | while | flops 2 | bytes 131181 | solution.py:108
  177.1 19.9 %custom-call.14 = f32[2,128,128]{1,2,0:T(8,128)S(1)} custom-call(f32[2,128,128]{2,1,0:T(8,128)S(1)} %get-tuple-element.18), custom_call_target="InvertDiagBlocksLowerTriangular" | custom-call | tf_op jit(solution)/shard_map/jit(_solve_triangular)/triangular_solve | solution.py:108
  199.3 5.1 %convolution_convert_fusion = bf16[3200,256]{1,0:T(8,128)(2,1)S(1)} fusion(bf16[3200,1024]{1,0:T(8,128)(2,1)} %copy-done.1, bf16[128,1024]{1,0:T(8,128)(2,1)S(1)} %fusion.15, f32[128,1024]{1,0:T(8,128)S(1)} %fusion.3), kind=kOutput, calls=%fused_computation.5 | convolution fusion | flops 1679589376 | bytes 8978432 | tf_op jit(solution)/shard_map/dot_general | solution.py:91
  204.4 23.9 %all_to_all.85 = bf16[16,200,256]{2,1,0:T(8,128)(2,1)S(1)} all-to-all(bf16[16,200,256]{2,1,0:T(8,128)(2,1)S(1)} %bitcast.125), channel_id=1, replica_groups=mesh['img_0'=8,'img_1'=2,'pix'=16] {'pix'}, dimensions={0} | all-to-all | bytes 3276800 | tf_op jit(solution)/shard_map/all_to_all | solution.py:18
  228.8 22.5 %all_to_all.86 = bf16[16,200,256]{2,1,0:T(8,128)(2,1)S(1)} all-to-all(bf16[16,200,256]{2,1,0:T(8,128)(2,1)S(1)} %broadcast_in_dim.21), channel_id=1, replica_groups=mesh['img_0'=8,'img_1'=2,'pix'=16] {'pix'}, dimensions={0} | all-to-all | bytes 3276800 | tf_op jit(solution)/shard_map/all_to_all | solution.py:24
  253.3 9.0 %all_to_all.87 = bf16[2,8,64,256]{3,2,1,0:T(8,128)(2,1)S(1)} all-to-all(bf16[2,8,64,256]{3,2,1,0:T(8,128)(2,1)S(1)} %bitcast.121), channel_id=1, replica_groups=mesh['img_0'=8,'img_1'=2,'pix'=16] {'img_1'}, dimensions={0} | all-to-all | bytes 1048576 | tf_op jit(solution)/shard_map/all_to_all | solution.py:18
  262.5 14.7 %all_to_all.88 = bf16[8,64,256]{2,1,0:T(8,128)(2,1)S(1)} all-to-all(bf16[8,64,256]{2,1,0:T(8,128)(2,1)S(1)} %reduce_sum.89), channel_id=1, replica_groups=mesh['img_0'=8,'img_1'=2,'pix'=16] {'img_0'}, dimensions={0} | all-to-all | bytes 524288 | tf_op jit(solution)/shard_map/all_to_all | solution.py:42
  277.3 14.2 %all_to_all.89 = bf16[8,64,256]{2,1,0:T(8,128)(2,1)S(1)} all-to-all(bf16[8,64,256]{2,1,0:T(8,128)(2,1)S(1)} %broadcast_in_dim.22), channel_id=1, replica_groups=mesh['img_0'=8,'img_1'=2,'pix'=16] {'img_0'}, dimensions={0} | all-to-all | bytes 524288 | tf_op jit(solution)/shard_map/all_to_all | solution.py:24
  291.5 4.8 %all_to_all.90 = bf16[2,8,64,256]{3,2,1,0:T(8,128)(2,1)S(1)} all-to-all(bf16[2,8,64,256]{3,2,1,0:T(8,128)(2,1)S(1)} %broadcast_in_dim.23), channel_id=1, replica_groups=mesh['img_0'=8,'img_1'=2,'pix'=16] {'img_1'}, dimensions={0} | all-to-all | bytes 1048576 | tf_op jit(solution)/shard_map/all_to_all | solution.py:24
  296.9 10.5 %all_to_all.91 = f32[16,16,256]{2,1,0:T(8,128)S(1)} all-to-all(f32[16,16,256]{2,1,0:T(8,128)S(1)} %fusion.29), channel_id=1, replica_groups=mesh['img_0'=8,'img_1'=2,'pix'=16] {'pix'}, dimensions={0} | all-to-all | bytes 524288 | tf_op jit(solution)/shard_map/all_to_all | solution.py:70
  308.2 4.1 %all-to-all-start.15 = ((f32[16,16,256]{2,1,0:T(8,128)}), f32[16,16,256]{2,1,0:T(8,128)S(1)}, u32[]{:S(2)}, u32[]{:S(2)}) async-start(f32[16,16,256]{2,1,0:T(8,128)} %broadcast_in_dim.24), calls=%async_computation.15 | async-start | bytes 524288 | tf_op jit(solution)/shard_map/all_to_all | solution.py:24
  312.4 7.2 %all-to-all-done.15 = f32[16,16,256]{2,1,0:T(8,128)S(1)} async-done(((f32[16,16,256]{2,1,0:T(8,128)}), f32[16,16,256]{2,1,0:T(8,128)S(1)}, u32[]{:S(2)}, u32[]{:S(2)}) %all-to-all-start.15) | async-done | bytes 262176 | tf_op jit(solution)/shard_map/all_to_all | solution.py:24
  319.8 11.7 %cholesky.164 = f32[128,128]{1,0:T(8,128)S(1)} custom-call(f32[128,128]{1,0:T(8,128)S(1)} %cholesky.197), custom_call_target="Cholesky" | custom-call | tf_op jit(solution)/shard_map/jit(cholesky)/cholesky | solution.py:107
  331.6 9.8 %custom-call.15 = f32[1,128,128]{1,2,0:T(8,128)S(1)} custom-call(f32[1,128,128]{2,1,0:T(8,128)S(1)} %get-tuple-element.53), custom_call_target="InvertDiagBlocksLowerTriangular" | custom-call | tf_op jit(solution)/shard_map/jit(cholesky)/cholesky | solution.py:107
  341.9 11.7 %cholesky.181 = f32[128,128]{1,0:T(8,128)S(1)} custom-call(f32[128,128]{1,0:T(8,128)S(1)} %convolution_subtract_fusion.2), custom_call_target="Cholesky" | custom-call | tf_op jit(solution)/shard_map/jit(cholesky)/cholesky | solution.py:107
  357.1 4.1 %while.5 = (s32[]{:T(128)}, f32[256,256]{1,0:T(8,128)S(1)}, s32[2,2]{1,0:T(2,128)S(1)}, f32[2,128,128]{2,1,0:T(8,128)S(1)}, s32[]{:T(128)}) while((s32[]{:T(128)}, f32[256,256]{1,0:T(8,128)S(1)}, s32[2,2]{1,0:T(2,128)S(1)}, f32[2,128,128]{2,1,0:T(8,128)S(1)}, s32[]{:T(128)}) %tuple.58), condition=%wide.while_cond.clone, body=%wide.while_body.clone.sunk | while | flops 2 | bytes 131181 | solution.py:108
  361.2 19.8 %custom-call.16 = f32[2,128,128]{1,2,0:T(8,128)S(1)} custom-call(f32[2,128,128]{2,1,0:T(8,128)S(1)} %get-tuple-element.19), custom_call_target="InvertDiagBlocksLowerTriangular" | custom-call | tf_op jit(solution)/shard_map/jit(_solve_triangular)/triangular_solve | solution.py:108
  (90 shorter events, 32.0 us)
Async XLA Ops:
  0.6 0.9 copy-start
  0.6 5.2 %copy-start.3 = (f32[1024,256]{1,0:T(8,128)S(1)}, f32[1024,256]{1,0:T(8,128)}, u32[]{:S(2)}) copy-start(f32[1024,256]{1,0:T(8,128)} %param.12) | copy-start | bytes 3145732
  5.9 3.2 copy-start.1
  9.1 29.0 %all-to-all-start = ((bf16[16,200,256]{2,1,0:T(8,128)(2,1)}), bf16[16,200,256]{2,1,0:T(8,128)(2,1)S(1)}, u32[]{:S(2)}, u32[]{:S(2)}) async-start(bf16[16,200,256]{2,1,0:T(8,128)(2,1)} %bitcast), calls=%async_computation | async-start | bytes 3276800 | tf_op jit(solution)/shard_map/all_to_all | solution.py:18
  38.0 26.6 %copy-start.2 = (bf16[3200,1024]{1,0:T(8,128)(2,1)S(1)}, bf16[3200,1024]{1,0:T(8,128)(2,1)}, u32[]{:S(2)}) copy-start(bf16[3200,1024]{1,0:T(8,128)(2,1)} %copy-done.1) | copy-start | bytes 19660804
  113.7 11.2 %all-to-all-start.6 = ((f32[16,16,256]{2,1,0:T(8,128)}), f32[16,16,256]{2,1,0:T(8,128)S(1)}, u32[]{:S(2)}, u32[]{:S(2)}) async-start(f32[16,16,256]{2,1,0:T(8,128)} %fusion.28), calls=%async_computation.6 | async-start | bytes 524288 | tf_op jit(solution)/shard_map/all_to_all | solution.py:70
  125.7 11.3 %all-to-all-start.7 = ((f32[16,16,256]{2,1,0:T(8,128)}), f32[16,16,256]{2,1,0:T(8,128)S(1)}, u32[]{:S(2)}, u32[]{:S(2)}) async-start(f32[16,16,256]{2,1,0:T(8,128)} %broadcast_in_dim.19), calls=%async_computation.7 | async-start | bytes 524288 | tf_op jit(solution)/shard_map/all_to_all | solution.py:24
  198.7 52.6 %slice-start = ((s8[6553600]{0:T(1024)(128)(4,1)}), s8[4194304]{0:T(1024)(128)(4,1)S(1)}, s32[]{:S(2)}) async-start(s8[6553600]{0:T(1024)(128)(4,1)} %bitcast.107), calls=%async_computation.16 | async-start | bytes 8388608
  199.3 52.0 %slice-start.1 = ((s8[6553600]{0:T(1024)(128)(4,1)}), s8[2359296]{0:T(1024)(128)(4,1)S(1)}, s32[]{:S(2)}) async-start(s8[6553600]{0:T(1024)(128)(4,1)} %bitcast.107), calls=%async_computation.17 | async-start | bytes 4718592
  308.2 11.4 %all-to-all-start.15 = ((f32[16,16,256]{2,1,0:T(8,128)}), f32[16,16,256]{2,1,0:T(8,128)S(1)}, u32[]{:S(2)}, u32[]{:S(2)}) async-start(f32[16,16,256]{2,1,0:T(8,128)} %broadcast_in_dim.24), calls=%async_computation.15 | async-start | bytes 524288 | tf_op jit(solution)/shard_map/all_to_all | solution.py:24
where the time goes:
time: 392 us; the launch traced here: 385 us
  blocking collectives  171 us (44%)
  other arithmetic  111 us (28%)
  waiting for transfers between devices  42.7 us (11%)
  matrix products  23.3 us (6%)
  starting transfers between devices  19.3 us (5%)
  local copies, waits for them, and re-layouts  13.7 us (3%)
    all_to_all x6, blocking collectives, sent_to_all(): lax.all_to_all(jnp.broadcast_to(x[None], (devices, *x.shape)), axis, 0, 0...  86.7 us
    another operation x13, other arithmetic, per_device(): factor = jnp.linalg.cholesky(gram_matrix)  68.7 us
    another operation x5, other arithmetic, per_device(): jax.scipy.linalg.solve_triangular(factor, image_sum.T, lower=True)  40.5 us
    all_to_all x3, blocking collectives, summed_on_arrival(): lax.all_to_all(blocks, axis, split_axis=0, concat_axis=0, tiled=True)  40.4 us
    all_to_all x2, blocking collectives, sum_in_two_steps(): lax.all_to_all(own.astype(jnp.bfloat16), far, 0, 0, tiled=True)  33.8 us
    all_to_all x1, waiting for transfers between devices, summed_on_arrival(): lax.all_to_all(blocks, axis, split_axis=0, concat_axis=0, tiled=True)  20.6 us
    all_to_all x2, waiting for transfers between devices, sent_to_all(): lax.all_to_all(jnp.broadcast_to(x[None], (devices, *x.shape)), axis, 0, 0...  14.4 us
    all_to_all x1, blocking collectives, summed_on_arrival_2(): blocks = lax.all_to_all(cut_along(x, dim, devices), axis, 0, 0, tiled=True)  10.5 us
  transfers between devices with their start and end apart: 4, of which 4 were waited for; matrix products, arithmetic and copies ran while one was open for 0% of the time, Pallas kernels for 0%

commit v1 on v0

--- a/solution.py
+++ b/solution.py
@@ -1,11 +1,93 @@
 import jax
 import jax.numpy as jnp
 from jax import lax
+from jax.experimental import pallas as pl
+from jax.experimental.pallas import tpu as pltpu
 from jax.sharding import Mesh
 from jax.sharding import PartitionSpec as P
 
 ITERS = 2
 IMG = ("img_0", "img_1")
+
+HIGHEST = lax.Precision.HIGHEST
+UP = float(2.0**24)
+DOWN = float(2.0**-24)
+
+def product(a, b, dims=((1,), (0,))):
+    return lax.dot_general(a, b, (dims, ((), ())), precision=HIGHEST, preferred_element_type=jnp.float32)
+
+
+def factor_blocks(gram, work, spread, small, inverse, upper):
+    pair, n = gram.shape[0], gram.shape[1]
+    work[...] = gram[...]
+    lane = lax.broadcasted_iota(jnp.int32, (pair, 128), 1)
+    col = lax.broadcasted_iota(jnp.int32, (16, n), 1)
+    for start in range(0, n, 16):
+        chunk = start // 128 * 128
+        off = start - chunk
+        for g in range(pair):
+            block = work[g, start : start + 16, chunk : chunk + 128]
+            for j in range(16):
+                spread[j, 16 * g : 16 * g + 16, :] = jnp.broadcast_to(block[:, off + j : off + j + 1], (16, 128))
+        a = {(i, j): spread[j, pl.ds(i, pair, stride=16), :] for j in range(16) for i in range(j, 16)}
+        inv = []
+        t = {}
+        for j in range(16):
+            root = lax.rsqrt(a[j, j])
+            inv.append(root)
+            for i in range(j + 1, 16):
+                a[i, j] = a[i, j] * root
+            for m in range(j + 1, 16):
+                for i in range(m, 16):
+                    a[i, m] = a[i, m] - a[i, j] * a[m, j]
+            t[j, j] = root
+            row = jnp.where(lane == off + j, root, 0.0)
+            for m in range(j):
+                total = a[j, m] * t[m, m]
+                for q in range(m + 1, j):
+                    total = total + a[j, q] * t[q, m]
+                t[j, m] = -root * total
+                row = jnp.where(lane == off + m, t[j, m], row)
+            small[pl.ds(j, pair, stride=16), :] = row
+        for g in range(pair):
+            head = small[16 * g : 16 * g + 16, :]
+            lead = product(head, work[g, chunk : chunk + 128, :])
+            wide = jnp.concatenate([head, head], axis=1) if n == 256 else head
+            here = (col >= start) & (col < start + 16)
+            mixed = jnp.where(here, wide, lead)
+            inverse[g, start : start + 16, :] = jnp.where(col < start + 16, mixed, 0.0)
+            upper[g, start : start + 16, :] = jnp.where(
+                col >= start + lax.broadcasted_iota(jnp.int32, (16, n), 0), lead, 0.0)
+            below = start + 16
+            if below < n:
+                side = product(work[g, below:, chunk : chunk + 128], head, ((1,), (1,)))
+                cols = lax.broadcasted_iota(jnp.int32, (n - below, n), 1)
+                old = work[g, below:, :]
+                old = jnp.where((cols >= start) & (cols < below), 0.0, old)
+                work[g, below:, :] = old - product(side, mixed)
+
+
+def finish_kernel(image_sum, gram, basis, factor, work, spread, small, inverse, upper):
+    factor_blocks(gram, work, spread, small, inverse, upper)
+    basis[...] = product(image_sum[...].astype(jnp.float32), inverse[1], ((1,), (1,)))
+    factor[...] = UP * product(inverse[0], upper[1], ((1,), (1,)))
+
+
+def finish(image_sum, gram):
+    rows, n = image_sum.shape
+    return pl.pallas_call(
+        finish_kernel,
+        out_shape=(jax.ShapeDtypeStruct((rows, n), jnp.float32), jax.ShapeDtypeStruct((n, n), jnp.float32)),
+        in_specs=[pl.BlockSpec(memory_space=pltpu.VMEM)] * 2,
+        out_specs=[pl.BlockSpec(memory_space=pltpu.VMEM)] * 2,
+        scratch_shapes=[
+            pltpu.VMEM((2, n, n), jnp.float32),
+            pltpu.VMEM((16, 32, 128), jnp.float32),
+            pltpu.VMEM((32, 128), jnp.float32),
+            pltpu.VMEM((2, n, n), jnp.float32),
+            pltpu.VMEM((2, n, n), jnp.float32),
+        ],
+    )(image_sum, gram)
 
 
 def cut_along(x, dim, devices):
@@ -78,35 +160,33 @@
     return lax.slice_in_dim(whole, 0, len(lines)).reshape(x.shape)
 
 
+def power_step(filtered, weight_share, probe_half):
+    shares = summed_on_arrival(
+        jnp.dot(filtered, probe_half, preferred_element_type=jnp.float32).astype(jnp.bfloat16),
+        "pix",
+        0,
+    )
+    scaled_share = (weight_share[:, None] * shares).astype(jnp.bfloat16)
+    scaled = collect(scaled_share, "pix", 0)
+    partial_sum = lax.dot_general(
+        filtered, scaled, (((0,), (0,)), ((), ())), preferred_element_type=jnp.float32
+    )
+    return sum_by_parts(partial_sum.astype(jnp.bfloat16), ("img_0", "img_1"))
+
+
 def per_device(images, classes, ctf_table, weights, probes):
     onehot = (classes[:, None] == jnp.arange(ctf_table.shape[0])[None, :]).astype(jnp.bfloat16)
     filters = jnp.dot(onehot, ctf_table, preferred_element_type=jnp.float32)
     filtered = (images.astype(jnp.float32) * filters).astype(jnp.bfloat16)
-    current = probes
-    factor = jnp.zeros((probes.shape[1], probes.shape[1]), jnp.float32)
-    for sweep in range(ITERS):
-        probe_half = current.astype(jnp.bfloat16)
-        share_rows = filtered.shape[0] // lax.axis_size("pix")
-        shares = summed_on_arrival(
-            jnp.dot(filtered, probe_half, preferred_element_type=jnp.float32).astype(jnp.bfloat16),
-            "pix",
-            0,
-        )
-        weight_share = lax.dynamic_slice_in_dim(
-            weights, lax.axis_index("pix") * share_rows, share_rows, 0
-        )
-        scaled_share = (weight_share[:, None] * shares).astype(jnp.bfloat16)
-        scaled = collect(scaled_share, "pix", 0)
-        partial_sum = lax.dot_general(
-            filtered, scaled, (((0,), (0,)), ((), ())), preferred_element_type=jnp.float32
-        )
-        image_sum = sum_by_parts(partial_sum.astype(jnp.bfloat16), ("img_0", "img_1"))
-        gram_matrix = sum_by_parts_2(
-            jnp.dot(image_sum.T, image_sum, precision=lax.Precision.HIGHEST), "pix"
-        )
-        factor = jnp.linalg.cholesky(gram_matrix)
-        current = jax.scipy.linalg.solve_triangular(factor, image_sum.T, lower=True).T
-    return (current, factor)
+    share_rows = filtered.shape[0] // lax.axis_size("pix")
+    weight_share = lax.dynamic_slice_in_dim(
+        weights, lax.axis_index("pix") * share_rows, share_rows, 0
+    )
+    first = power_step(filtered, weight_share, probes.astype(jnp.bfloat16))
+    second = power_step(filtered, weight_share, (first * DOWN).astype(jnp.bfloat16))
+    grams = jnp.stack([jnp.dot(s.T, s, precision=HIGHEST) for s in (first, second)])
+    gram = sum_by_parts_2(grams, "pix")
+    return finish(second, gram)
 
 
 def solution(mesh):

time: 392 us -> 268 us (0.68); the launches traced: 385 us -> 266 us
  other arithmetic: 111 us -> 2.24 us
  Pallas kernels: 0 us -> 25.2 us
  local copies, waits for them, and re-layouts: 13.7 us -> 4.51 us
  blocking collectives: 171 us -> 162 us
  matrix products: 23.3 us -> 17 us
  starting transfers between devices: 19.3 us -> 14.9 us
    another operation x18 -> x1, other arithmetic: 109 us -> 0.04 us  [per_device(): jnp.stack([jnp.dot(s.T, s, precision=HIGHEST) for s in (first, second)])]
    pallas_call x0 -> x1, Pallas kernels: none -> 25.2 us  [finish(): pl.pallas_call(finish_kernel, out_shape=(jax.ShapeDtypeStruct((rows, n),...]
    all_to_all x6 -> x5, blocking collectives: 86.7 us -> 74.6 us  [sent_to_all(): lax.all_to_all(jnp.broadcast_to(x[None], (devices, *x.shape)), axis, 0, 0...]
    another operation x19 -> x0, local copies, waits for them, and re-layouts: 8.06 us -> none  [the longest x15 8.01 us: per_device(): jax.scipy.linalg.solve_triangular(factor, image_sum.T, lower=True)]
    all_to_all x1 -> x0, waiting for transfers between devices: 7.69 us -> none  [summed_on_arrival_2(): blocks = lax.all_to_all(cut_along(x, dim, devices), axis, 0, 0, tiled=True)]
    another operation x10 -> x0, matrix products: 5.49 us -> none  [the longest x6 4.55 us: per_device(): jax.scipy.linalg.solve_triangular(factor, image_sum.T, lower=True)]
    all_to_all x2, waiting for transfers between devices: 14.4 us -> 19.3 us  [sent_to_all(): lax.all_to_all(jnp.broadcast_to(x[None], (devices, *x.shape)), axis, 0, 0...]
  transfers between devices with their start and end apart: 4 -> 3, of which waited for: 4 -> 3; matrix products, arithmetic and copies ran while one was open for 0% -> 1% of each run, Pallas kernels for 0% -> 0%
where the time goes in v1:
time: 268 us; the launch traced here: 266 us
  blocking collectives  162 us (60%)
  waiting for transfers between devices  39.9 us (15%)
  Pallas kernels  25.2 us (9%)
  matrix products  17 us (6%)
  starting transfers between devices  14.9 us (6%)
  local copies, waits for them, and re-layouts  4.51 us (2%)
    all_to_all x5, blocking collectives, sent_to_all(): lax.all_to_all(jnp.broadcast_to(x[None], (devices, *x.shape)), axis, 0, 0...  74.6 us
    all_to_all x3, blocking collectives, summed_on_arrival(): lax.all_to_all(blocks, axis, split_axis=0, concat_axis=0, tiled=True)  39.8 us
    all_to_all x2, blocking collectives, sum_in_two_steps(): lax.all_to_all(own.astype(jnp.bfloat16), far, 0, 0, tiled=True)  33.8 us
    pallas_call x1, Pallas kernels, finish(): pl.pallas_call(finish_kernel, out_shape=(jax.ShapeDtypeStruct((rows, n),...  25.2 us
    all_to_all x1, waiting for transfers between devices, summed_on_arrival(): lax.all_to_all(blocks, axis, split_axis=0, concat_axis=0, tiled=True)  20.6 us
    all_to_all x2, waiting for transfers between devices, sent_to_all(): lax.all_to_all(jnp.broadcast_to(x[None], (devices, *x.shape)), axis, 0, 0...  19.3 us
    all_to_all x1, blocking collectives, summed_on_arrival_2(): blocks = lax.all_to_all(cut_along(x, dim, devices), axis, 0, 0, tiled=True)  13.3 us
    dot_general x2, matrix products, power_step(): jnp.dot(filtered, probe_half, preferred_element_type=jnp.float32)  8.05 us
  transfers between devices with their start and end apart: 3, of which 3 were waited for; matrix products, arithmetic and copies ran while one was open for 1% of the time, Pallas kernels for 0%

profile of v1, /device:TPU:1, one launch (start us, length us, event | category | flops | bytes accessed | tf_op | source)
XLA Modules:
  0.0 266.1 jit_solution(11144469349179486167)
XLA Ops:
  0.7 0.9 copy-done
  1.5 4.3 %multiply_convert_fusion = bf16[3200,1024]{1,0:T(8,128)(2,1)S(1)} fusion(bf16[3200,1024]{1,0:T(8,128)(2,1)} %param.5, bf16[64,1024]{1,0:T(8,128)(2,1)S(1)} %copy-done, s32[3200]{0:T(1024)} %param.6), kind=kOutput, calls=%fused_computation | convolution fusion | flops 429465600 | bytes 13251072 | tf_op jit(solution)/shard_map/dot_general | solution.py:179
  5.9 3.2 %convolution_convert_fusion.1 = bf16[3200,256]{1,0:T(8,128)(2,1)} fusion(bf16[3200,1024]{1,0:T(8,128)(2,1)S(1)} %multiply_convert_fusion, f32[1024,256]{1,0:T(8,128)S(1)} %copy-done.4), kind=kOutput, calls=%fused_computation.2 | convolution fusion | flops 1678802944 | bytes 9240576 | tf_op jit(solution)/shard_map/dot_general | solution.py:165
  9.0 7.6 %all-to-all-start = ((bf16[16,200,256]{2,1,0:T(8,128)(2,1)}), bf16[16,200,256]{2,1,0:T(8,128)(2,1)S(1)}, u32[]{:S(2)}, u32[]{:S(2)}) async-start(bf16[16,200,256]{2,1,0:T(8,128)(2,1)} %bitcast), calls=%async_computation | async-start | bytes 3276800 | tf_op jit(solution)/shard_map/all_to_all | solution.py:100
  16.6 0.8 dynamic_slice.3
  17.4 20.6 %all-to-all-done = bf16[16,200,256]{2,1,0:T(8,128)(2,1)S(1)} async-done(((bf16[16,200,256]{2,1,0:T(8,128)(2,1)}), bf16[16,200,256]{2,1,0:T(8,128)(2,1)S(1)}, u32[]{:S(2)}, u32[]{:S(2)}) %all-to-all-start) | async-done | bytes 1638432 | tf_op jit(solution)/shard_map/all_to_all | solution.py:100
  38.5 26.2 %all_to_all.70 = bf16[16,200,256]{2,1,0:T(8,128)(2,1)S(1)} all-to-all(bf16[16,200,256]{2,1,0:T(8,128)(2,1)S(1)} %broadcast_in_dim.14), channel_id=1, replica_groups=mesh['img_0'=8,'img_1'=2,'pix'=16] {'pix'}, dimensions={0} | all-to-all | bytes 3276800 | tf_op jit(solution)/shard_map/all_to_all | solution.py:106
  64.7 2.0 convolution_convert_fusion.3
  66.7 7.5 %all_to_all.71 = bf16[2,8,64,256]{3,2,1,0:T(8,128)(2,1)S(1)} all-to-all(bf16[2,8,64,256]{3,2,1,0:T(8,128)(2,1)S(1)} %bitcast.54), channel_id=1, replica_groups=mesh['img_0'=8,'img_1'=2,'pix'=16] {'img_1'}, dimensions={0} | all-to-all | bytes 1048576 | tf_op jit(solution)/shard_map/all_to_all | solution.py:100
  74.3 19.1 %all_to_all.72 = bf16[8,64,256]{2,1,0:T(8,128)(2,1)S(1)} all-to-all(bf16[8,64,256]{2,1,0:T(8,128)(2,1)S(1)} %reduce_sum.76), channel_id=1, replica_groups=mesh['img_0'=8,'img_1'=2,'pix'=16] {'img_0'}, dimensions={0} | all-to-all | bytes 524288 | tf_op jit(solution)/shard_map/all_to_all | solution.py:124
  93.4 12.2 %all_to_all.73 = bf16[8,64,256]{2,1,0:T(8,128)(2,1)S(1)} all-to-all(bf16[8,64,256]{2,1,0:T(8,128)(2,1)S(1)} %broadcast_in_dim.15), channel_id=1, replica_groups=mesh['img_0'=8,'img_1'=2,'pix'=16] {'img_0'}, dimensions={0} | all-to-all | bytes 524288 | tf_op jit(solution)/shard_map/all_to_all | solution.py:106
  105.6 6.8 %all_to_all.74 = bf16[2,8,64,256]{3,2,1,0:T(8,128)(2,1)S(1)} all-to-all(bf16[2,8,64,256]{3,2,1,0:T(8,128)(2,1)S(1)} %broadcast_in_dim.16), channel_id=1, replica_groups=mesh['img_0'=8,'img_1'=2,'pix'=16] {'img_1'}, dimensions={0} | all-to-all | bytes 1048576 | tf_op jit(solution)/shard_map/all_to_all | solution.py:106
  112.6 4.9 %convolution_convert_fusion = bf16[3200,256]{1,0:T(8,128)(2,1)S(1)} fusion(bf16[3200,1024]{1,0:T(8,128)(2,1)} %copy-done.1, bf16[1024,256]{1,0:T(8,128)(2,1)S(1)} %bitcast.57), kind=kOutput, calls=%fused_computation.1 | convolution fusion | flops 1678540800 | bytes 8716288 | tf_op jit(solution)/shard_map/dot_general | solution.py:165
  117.5 25.7 %all_to_all.75 = bf16[16,200,256]{2,1,0:T(8,128)(2,1)S(1)} all-to-all(bf16[16,200,256]{2,1,0:T(8,128)(2,1)S(1)} %bitcast.56), channel_id=1, replica_groups=mesh['img_0'=8,'img_1'=2,'pix'=16] {'pix'}, dimensions={0} | all-to-all | bytes 3276800 | tf_op jit(solution)/shard_map/all_to_all | solution.py:100
  143.2 0.2 convert_reduce_fusion
  143.7 24.7 %all_to_all.76 = bf16[16,200,256]{2,1,0:T(8,128)(2,1)S(1)} all-to-all(bf16[16,200,256]{2,1,0:T(8,128)(2,1)S(1)} %broadcast_in_dim.17), channel_id=1, replica_groups=mesh['img_0'=8,'img_1'=2,'pix'=16] {'pix'}, dimensions={0} | all-to-all | bytes 3276800 | tf_op jit(solution)/shard_map/all_to_all | solution.py:106
  168.3 2.0 convolution_convert_fusion.2
  170.3 6.6 %all_to_all.77 = bf16[2,8,64,256]{3,2,1,0:T(8,128)(2,1)S(1)} all-to-all(bf16[2,8,64,256]{3,2,1,0:T(8,128)(2,1)S(1)} %bitcast.55), channel_id=1, replica_groups=mesh['img_0'=8,'img_1'=2,'pix'=16] {'img_1'}, dimensions={0} | all-to-all | bytes 1048576 | tf_op jit(solution)/shard_map/all_to_all | solution.py:100
  177.1 14.7 %all_to_all.78 = bf16[8,64,256]{2,1,0:T(8,128)(2,1)S(1)} all-to-all(bf16[8,64,256]{2,1,0:T(8,128)(2,1)S(1)} %reduce_sum.79), channel_id=1, replica_groups=mesh['img_0'=8,'img_1'=2,'pix'=16] {'img_0'}, dimensions={0} | all-to-all | bytes 524288 | tf_op jit(solution)/shard_map/all_to_all | solution.py:124
  191.9 0.7 broadcast_in_dim.18
  192.6 3.4 %all-to-all-start.10 = ((bf16[8,64,256]{2,1,0:T(8,128)(2,1)}), bf16[8,64,256]{2,1,0:T(8,128)(2,1)S(1)}, u32[]{:S(2)}, u32[]{:S(2)}) async-start(bf16[8,64,256]{2,1,0:T(8,128)(2,1)} %broadcast_in_dim.18), calls=%async_computation.10 | async-start | bytes 524288 | tf_op jit(solution)/shard_map/all_to_all | solution.py:106
  196.0 0.3 convolution_bitcast_fusion.1
  196.3 11.4 %all-to-all-done.10 = bf16[8,64,256]{2,1,0:T(8,128)(2,1)S(1)} async-done(((bf16[8,64,256]{2,1,0:T(8,128)(2,1)}), bf16[8,64,256]{2,1,0:T(8,128)(2,1)S(1)}, u32[]{:S(2)}, u32[]{:S(2)}) %all-to-all-start.10) | async-done | bytes 262176 | tf_op jit(solution)/shard_map/all_to_all | solution.py:106
  207.8 4.8 %all_to_all.79 = bf16[2,8,64,256]{3,2,1,0:T(8,128)(2,1)S(1)} all-to-all(bf16[2,8,64,256]{3,2,1,0:T(8,128)(2,1)S(1)} %broadcast_in_dim.19), channel_id=1, replica_groups=mesh['img_0'=8,'img_1'=2,'pix'=16] {'img_1'}, dimensions={0} | all-to-all | bytes 1048576 | tf_op jit(solution)/shard_map/all_to_all | solution.py:106
  212.6 0.3 convolution_bitcast_fusion
  213.0 13.3 %all_to_all.80 = f32[16,32,256]{2,1,0:T(8,128)S(1)} all-to-all(f32[16,32,256]{2,1,0:T(8,128)S(1)} %bitcast.53), channel_id=1, replica_groups=mesh['img_0'=8,'img_1'=2,'pix'=16] {'pix'}, dimensions={0} | all-to-all | bytes 1048576 | tf_op jit(solution)/shard_map/all_to_all | solution.py:152
  226.3 0.8 broadcast_in_dim.20
  227.2 3.9 %all-to-all-start.13 = ((f32[16,32,256]{2,1,0:T(8,128)}), f32[16,32,256]{2,1,0:T(8,128)S(1)}, u32[]{:S(2)}, u32[]{:S(2)}) async-start(f32[16,32,256]{2,1,0:T(8,128)} %broadcast_in_dim.20), calls=%async_computation.13 | async-start | bytes 1048576 | tf_op jit(solution)/shard_map/all_to_all | solution.py:106
  231.1 1.1 bitcast_convert_fusion.image_sum
  232.2 7.9 %all-to-all-done.13 = f32[16,32,256]{2,1,0:T(8,128)S(1)} async-done(((f32[16,32,256]{2,1,0:T(8,128)}), f32[16,32,256]{2,1,0:T(8,128)S(1)}, u32[]{:S(2)}, u32[]{:S(2)}) %all-to-all-start.13) | async-done | bytes 524320 | tf_op jit(solution)/shard_map/all_to_all | solution.py:106
  240.2 0.8 copy-done.3
  241.0 25.2 %shard_map.68 = (f32[1024,256]{1,0:T(8,128)}, f32[256,256]{1,0:T(8,128)}) custom-call(f32[1024,256]{1,0:T(8,128)} %bitcast_convert_fusion.image_sum, f32[2,256,256]{2,1,0:T(8,128)} %bitcast.50), custom_call_target="tpu_custom_call" | custom-call | tf_op jit(solution)/shard_map/pallas_call | solution.py:78
  (31 shorter events, 1.4 us)
Async XLA Ops:
  0.6 0.9 copy-start
  0.6 5.2 %copy-start.4 = (f32[1024,256]{1,0:T(8,128)S(1)}, f32[1024,256]{1,0:T(8,128)}, u32[]{:S(2)}) copy-start(f32[1024,256]{1,0:T(8,128)} %param.9) | copy-start | bytes 3145732
  5.9 3.2 %copy-start.1 = (bf16[3200,1024]{1,0:T(8,128)(2,1)}, bf16[3200,1024]{1,0:T(8,128)(2,1)S(1)}, u32[]{:S(2)}) copy-start(bf16[3200,1024]{1,0:T(8,128)(2,1)S(1)} %multiply_convert_fusion) | copy-start | bytes 19660804
  9.0 29.0 %all-to-all-start = ((bf16[16,200,256]{2,1,0:T(8,128)(2,1)}), bf16[16,200,256]{2,1,0:T(8,128)(2,1)S(1)}, u32[]{:S(2)}, u32[]{:S(2)}) async-start(bf16[16,200,256]{2,1,0:T(8,128)(2,1)} %bitcast), calls=%async_computation | async-start | bytes 3276800 | tf_op jit(solution)/shard_map/all_to_all | solution.py:100
  38.1 26.6 %copy-start.2 = (bf16[3200,1024]{1,0:T(8,128)(2,1)S(1)}, bf16[3200,1024]{1,0:T(8,128)(2,1)}, u32[]{:S(2)}) copy-start(bf16[3200,1024]{1,0:T(8,128)(2,1)} %copy-done.1) | copy-start | bytes 19660804
  112.5 55.8 %slice-start = ((s8[6553600]{0:T(1024)(128)(4,1)}), s8[4194304]{0:T(1024)(128)(4,1)S(1)}, s32[]{:S(2)}) async-start(s8[6553600]{0:T(1024)(128)(4,1)} %bitcast.46), calls=%async_computation.14 | async-start | bytes 8388608
  112.6 55.7 %slice-start.1 = ((s8[6553600]{0:T(1024)(128)(4,1)}), s8[2359296]{0:T(1024)(128)(4,1)S(1)}, s32[]{:S(2)}) async-start(s8[6553600]{0:T(1024)(128)(4,1)} %bitcast.46), calls=%async_computation.15 | async-start | bytes 4718592
  192.6 15.1 %all-to-all-start.10 = ((bf16[8,64,256]{2,1,0:T(8,128)(2,1)}), bf16[8,64,256]{2,1,0:T(8,128)(2,1)S(1)}, u32[]{:S(2)}, u32[]{:S(2)}) async-start(bf16[8,64,256]{2,1,0:T(8,128)(2,1)} %broadcast_in_dim.18), calls=%async_computation.10 | async-start | bytes 524288 | tf_op jit(solution)/shard_map/all_to_all | solution.py:106
  227.2 13.0 %all-to-all-start.13 = ((f32[16,32,256]{2,1,0:T(8,128)}), f32[16,32,256]{2,1,0:T(8,128)S(1)}, u32[]{:S(2)}, u32[]{:S(2)}) async-start(f32[16,32,256]{2,1,0:T(8,128)} %broadcast_in_dim.20), calls=%async_computation.13 | async-start | bytes 1048576 | tf_op jit(solution)/shard_map/all_to_all | solution.py:106
  240.1 0.8 copy-start.3

commit v2 on v1

v2 whole, which is shorter than its diff:
```python
import jax
import jax.numpy as jnp
from jax import lax
from jax.experimental import pallas as pl
from jax.experimental.pallas import tpu as pltpu
from jax.sharding import PartitionSpec as P

ITERS = 2

HIGHEST = lax.Precision.HIGHEST
UP = float(2.0**24)
DOWN = float(2.0**-24)

def product(a, b, dims=((1,), (0,))):
    return lax.dot_general(a, b, (dims, ((), ())), precision=HIGHEST, preferred_element_type=jnp.float32)


def factor_blocks(gram, work, spread, small, inverse, upper):
    pair, n = gram.shape[0], gram.shape[1]
    work[...] = gram[...]
    lane = lax.broadcasted_iota(jnp.int32, (pair, 128), 1)
    col = lax.broadcasted_iota(jnp.int32, (16, n), 1)
    for start in range(0, n, 16):
        chunk = start // 128 * 128
        off = start - chunk
        for g in range(pair):
            block = work[g, start : start + 16, chunk : chunk + 128]
            for j in range(16):
                spread[j, 16 * g : 16 * g + 16, :] = jnp.broadcast_to(block[:, off + j : off + j + 1], (16, 128))
        a = {(i, j): spread[j, pl.ds(i, pair, stride=16), :] for j in range(16) for i in range(j, 16)}
        inv = []
        t = {}
        for j in range(16):
            root = lax.rsqrt(a[j, j])
            inv.append(root)
            for i in range(j + 1, 16):
                a[i, j] = a[i, j] * root
            for m in range(j + 1, 16):
                for i in range(m, 16):
                    a[i, m] = a[i, m] - a[i, j] * a[m, j]
            t[j, j] = root
            row = jnp.where(lane == off + j, root, 0.0)
            for m in range(j):
                total = a[j, m] * t[m, m]
                for q in range(m + 1, j):
                    total = total + a[j, q] * t[q, m]
                t[j, m] = -root * total
                row = jnp.where(lane == off + m, t[j, m], row)
            small[pl.ds(j, pair, stride=16), :] = row
        for g in range(pair):
            head = small[16 * g : 16 * g + 16, :]
            lead = product(head, work[g, chunk : chunk + 128, :])
            wide = jnp.concatenate([head, head], axis=1) if n == 256 else head
            here = (col >= start) & (col < start + 16)
            mixed = jnp.where(here, wide, lead)
            inverse[g, start : start + 16, :] = jnp.where(col < start + 16, mixed, 0.0)
            upper[g, start : start + 16, :] = jnp.where(
                col >= start + lax.broadcasted_iota(jnp.int32, (16, n), 0), lead, 0.0)
            below = start + 16
            if below < n:
                side = product(work[g, below:, chunk : chunk + 128], head, ((1,), (1,)))
                cols = lax.broadcasted_iota(jnp.int32, (n - below, n), 1)
                old = work[g, below:, :]
                old = jnp.where((cols >= start) & (cols < below), 0.0, old)
                work[g, below:, :] = old - product(side, mixed)


def finish_kernel(image_sum, gram, basis, factor, work, spread, small, inverse, upper):
    factor_blocks(gram, work, spread, small, inverse, upper)
    basis[...] = product(inverse[1], image_sum[...].astype(jnp.float32)).T
    factor[...] = product(inverse[0], upper[1], ((1,), (1,)))


def finish(image_sum, gram):
    n, rows = image_sum.shape
    return pl.pallas_call(
        finish_kernel,
        out_shape=(jax.ShapeDtypeStruct((rows, n), jnp.float32), jax.ShapeDtypeStruct((n, n), jnp.float32)),
        in_specs=[pl.BlockSpec(memory_space=pltpu.VMEM)] * 2,
        out_specs=[pl.BlockSpec(memory_space=pltpu.VMEM)] * 2,
        scratch_shapes=[
            pltpu.VMEM((2, n, n), jnp.float32),
            pltpu.VMEM((16, 32, 128), jnp.float32),
            pltpu.VMEM((32, 128), jnp.float32),
            pltpu.VMEM((2, n, n), jnp.float32),
            pltpu.VMEM((2, n, n), jnp.float32),
        ],
    )(image_sum, gram)


SHARE_TILES = ((7, 6, 6, 6), (6, 6, 7, 6))
WIDTH = 128
MESH = pl.DeviceIdType.MESH


def remote(src, dst, send, recv, to):
    return pltpu.make_async_remote_copy(
        src_ref=src, dst_ref=dst, send_sem=send, recv_sem=recv, device_id=to, device_id_type=MESH)


class Place:
    def __init__(self):
        self.img, self.pix = lax.axis_index("img"), lax.axis_index("pix")
        self.z, self.core = self.img // 2, self.img % 2
        x, y = self.pix // 4, self.pix % 4
        self.bits, self.across = [], []
        for near, far in ((x, y), (y, x)):
            high, low = near // 2, near % 2
            self.bits.append(((high + low) % 2, high))
        flips = ((x + 1 - 2 * (x % 2)) * 4 + y, (3 - x) * 4 + y, x * 4 + y + 1 - 2 * (y % 2), x * 4 + 3 - y)
        (xv, xu), (yv, yu) = self.bits
        self.bits = (xv, yv, xu, yu)
        self.across = tuple((self.img, p) for p in (flips[0], flips[2], flips[1], flips[3]))
        self.partner = (self.z * 2 + 1 - self.core, self.pix)

    def along_z(self, d):
        return ((self.z + d) % 8 * 2 + self.core, self.pix)

    def in_plane(self, d):
        return (self.img, (self.pix + d) % 16)


def greet(here):
    barrier = pltpu.get_barrier_semaphore()
    peers = [here.in_plane(d) for d in range(1, 16)] + [here.along_z(d) for d in range(1, 8)] + [here.partner]
    for peer in peers:
        pl.semaphore_signal(barrier, inc=1, device_id=peer, device_id_type=MESH)
    pl.semaphore_wait(barrier, len(peers))


def tiles_of(c):
    first, streams = 0, []
    for share in SHARE_TILES[c]:
        streams.append((first, share))
        first += 16 * share
    return streams


def sweep(here, sends, t, c, filtered, weights, probe, scores, landed, scaled, shares, crossed, halves, arrived, whole, sems):
    rs_send, rs_recv, ag_send, ag_recv, d2d_send, d2d_recv, z_send, z_recv, g_send, g_recv, f_send, f_recv = sems
    streams = tiles_of(c)
    dims = ((1,), (0,)) if t == 0 else ((1,), (1,))

    def bit(s, i):
        return here.bits[(s + i) % 4]

    def across(s, i):
        return here.across[(s + i) % 4]

    start = [[first] for first, _ in streams]
    flow = [[None] * 4 for _ in streams]
    base = 0

    def score(first, tiles):
        rows = pl.ds(pl.multiple_of(first * 8, 64), tiles * 8)
        part = lax.dot_general(
            filtered[rows, :], probe(), (dims, ((), ())), preferred_element_type=jnp.float32)
        scores[pl.ds(first, tiles)] = part.reshape(tiles, 8, WIDTH).astype(jnp.bfloat16)

    def pass_half(s, i):
        share = streams[s][1]
        half = share * 16 >> (i + 1)
        off = start[s][i]
        give, keep = off + (1 - bit(s, i)) * half, off + bit(s, i) * half
        start[s].append(keep)
        return give, keep, half

    slots = []
    at = 0
    for i in range(4):
        for s in range(4):
            slots.append(at)
            at += streams[s][1] * 16 >> (i + 1)

    def send_half(s, i, give, half):
        flow[s][i] = remote(
            scores.at[pl.ds(give, half)], landed.at[pl.ds(slots[4 * i + s], half)],
            rs_send.at[i, s], rs_recv.at[i, s], across(s, i))
        flow[s][i].start()
        sends.append(flow[s][i])

    todo = []
    for s in range(4):
        give, keep, half = pass_half(s, 0)
        score(give, half)
        send_half(s, 0, give, half)
        todo.append((keep, half))
    for keep, half in todo:
        score(keep, half)
    for i in range(4):
        yield ("rs", t, i)
        for s in range(4):
            half = streams[s][1] * 16 >> (i + 1)
            keep = start[s][i + 1]
            flow[s][i].wait_recv()
            mine = scores[pl.ds(keep, half)].astype(jnp.float32)
            mine = mine + landed[pl.ds(slots[4 * i + s], half)].astype(jnp.float32)
            if i < 3:
                scores[pl.ds(keep, half)] = mine.astype(jnp.bfloat16)
                give, _, small = pass_half(s, i + 1)
                send_half(s, i + 1, give, small)
            else:
                scaled[pl.ds(keep, half)] = (weights[pl.ds(keep, half)] * mine).astype(jnp.bfloat16)
                flow[s][3] = None
    back = [[None] * 4 for _ in streams]

    def send_back(s, i):
        half = streams[s][1] * 16 >> (i + 1)
        own = scaled.at[pl.ds(start[s][i + 1], half)]
        back[s][i] = remote(own, own, ag_send.at[i, s], ag_recv.at[i, s], across(s, i))
        back[s][i].start()
        sends.append(back[s][i])

    for s in range(4):
        send_back(s, 3)
    for i in (3, 2, 1, 0):
        yield ("ag", t, 3 - i)
        for s in range(4):
            back[s][i].wait_recv()
            if i:
                send_back(s, i - 1)
    total = lax.dot_general(
        scaled[...].reshape(-1, WIDTH), filtered[...], (((0,), (0,)), ((), ())), preferred_element_type=jnp.float32)
    shares[...] = total.reshape(16, 8, -1).astype(jnp.bfloat16)
    swap = remote(shares.at[pl.ds((1 - here.core) * 8, 8)], crossed, d2d_send.at[0], d2d_recv.at[0], here.partner)
    swap.start()
    sends.append(swap)
    yield ("img", t, 0)
    swap.wait_recv()
    rounds = []
    for d in range(1, 8):
        k = (here.z + d) % 8
        pair = shares[here.core * 8 + k].astype(jnp.float32) + crossed[k].astype(jnp.float32)
        halves[d] = pair.astype(jnp.bfloat16)
        copy = remote(halves.at[d], arrived.at[d], z_send.at[d], z_recv.at[d], here.along_z(d))
        copy.start()
        rounds.append(copy)
    sends.extend(rounds)
    own = shares[here.core * 8 + here.z].astype(jnp.float32) + crossed[here.z].astype(jnp.float32)
    yield ("img", t, 1)
    for d, copy in enumerate(rounds, 1):
        copy.wait_recv()
        own = own + arrived[d].astype(jnp.float32)
    mine = here.core * 8 + here.z
    whole[mine] = own.astype(jnp.bfloat16)
    rounds = []
    for d in range(1, 8):
        copy = remote(whole.at[mine], whole.at[mine], g_send.at[d], g_recv.at[d], here.along_z(d))
        copy.start()
        rounds.append(copy)
    sends.extend(rounds)
    over = [remote(whole.at[mine], whole.at[mine], f_send.at[0], f_recv.at[0], here.partner)]
    over[0].start()
    yield ("img", t, 2)
    for d, copy in enumerate(rounds, 1):
        copy.wait_recv()
        k = here.core * 8 + (here.z + 8 - d) % 8
        fwd = remote(whole.at[k], whole.at[k], f_send.at[d], f_recv.at[d], here.partner)
        fwd.start()
        over.append(fwd)
    sends.extend(over)
    yield ("img", t, 3)
    for fwd in over:
        fwd.wait_recv()


def gram_sum(here, sends, basis, out, parts, landed, sems):
    r_send, r_recv, a_send, a_recv = sems
    gram = lax.dot_general(basis[...], basis[...], (((1,), (1,)), ((), ())), preferred_element_type=jnp.float32)
    parts[...] = gram.reshape(16, 16, -1)
    rounds = []
    for d in range(1, 16):
        copy = remote(parts.at[(here.pix + d) % 16], landed.at[d], r_send.at[d], r_recv.at[d], here.in_plane(d))
        copy.start()
        rounds.append(copy)
    sends.extend(rounds)
    own = parts[here.pix]
    yield ("gram", 0, 0)
    for d, copy in enumerate(rounds, 1):
        copy.wait_recv()
        own = own + landed[d]
    out[here.pix] = own
    rounds = []
    for d in range(1, 16):
        copy = remote(out.at[here.pix], out.at[here.pix], a_send.at[d], a_recv.at[d], here.in_plane(d))
        copy.start()
        rounds.append(copy)
    sends.extend(rounds)
    yield ("gram", 0, 1)
    for copy in rounds:
        copy.wait_recv()


def sweeps_kernel(
    filtered, weights, probes, basis, grams,
    scores, landed, scaled, shares, crossed, halves, arrived, whole, joined, parts, gram_landed, gram_whole,
    rs_send, rs_recv, ag_send, ag_recv, d2d_send, d2d_recv, z_send, z_recv, g_send, g_recv, f_send, f_recv,
    r_send, r_recv, a_send, a_recv,
):
    here = Place()
    greet(here)
    sends = []
    all_sems = (rs_send, rs_recv, ag_send, ag_recv, d2d_send, d2d_recv, z_send, z_recv, g_send, g_recv, f_send, f_recv)

    def run(c):
        cols = slice(c * WIDTH, (c + 1) * WIDTH)
        for t in range(ITERS):
            probe = (lambda: probes[:, cols]) if t == 0 else (lambda: joined[0, cols, :])
            n = 2 * t + c
            yield from sweep(
                here, sends, t, c, filtered, weights, probe, scores.at[n], landed.at[n], scaled.at[n], shares.at[n],
                crossed.at[n], halves.at[n], arrived.at[n], whole.at[n], [sem.at[n] for sem in all_sems])
            found = whole[n].reshape(WIDTH, -1)
            if t == 0:
                joined[0, cols, :] = (found.astype(jnp.float32) * DOWN).astype(jnp.bfloat16)
            else:
                basis[cols, :] = found

    def gram(t):
        sems = [sem.at[t] for sem in (r_send, r_recv, a_send, a_recv)]
        yield from gram_sum(
            here, sends, joined.at[0] if t == 0 else basis, gram_whole.at[t], parts.at[t], gram_landed.at[t], sems)

    live = [run(c) for c in range(2)]
    label = next(live[0])
    while label != LAG:
        label = next(live[0])
    pending = True
    while live:
        for one in list(live):
            label = next(one, None)
            if label is None:
                live.remove(one)
            elif label == ("img", 1, 0) and pending and one is live[-1]:
                pending = False
                live.append(gram(0))
    for _ in gram(1):
        pass
    grams[...] = gram_whole[...]
    for copy in sends:
        copy.wait_send()


LAG = ("rs", 0, 0)


def sweeps(filtered, weights, probes):
    rows, pixels = filtered.shape
    n = probes.shape[1]
    tiles = rows // 8
    four = 2 * ITERS
    bf16, f32 = jnp.bfloat16, jnp.float32
    dma = pltpu.SemaphoreType.DMA
    vmem = pl.BlockSpec(memory_space=pltpu.VMEM)
    return pl.pallas_call(
        sweeps_kernel,
        out_shape=(jax.ShapeDtypeStruct((n, pixels), bf16), jax.ShapeDtypeStruct((2, 16, 16, n), f32)),
        in_specs=[vmem] * 3,
        out_specs=[vmem] * 2,
        scratch_shapes=[
            pltpu.VMEM((four, tiles, 8, WIDTH), bf16),
            pltpu.VMEM((four, tiles * 15 // 16, 8, WIDTH), bf16),
            pltpu.VMEM((four, tiles, 8, WIDTH), bf16),
            pltpu.VMEM((four, 16, 8, pixels), bf16),
            pltpu.VMEM((four, 8, 8, pixels), bf16),
            pltpu.VMEM((four, 8, 8, pixels), bf16),
            pltpu.VMEM((four, 8, 8, pixels), bf16),
            pltpu.VMEM((four, 16, 8, pixels), bf16),
            pltpu.VMEM((1, n, pixels), bf16),
            pltpu.VMEM((2, 16, 16, n), f32),
            pltpu.VMEM((2, 16, 16, n), f32),
            pltpu.VMEM((2, 16, 16, n), f32),
            *[dma((four, 4, 4))] * 4,
            *[dma((four, 1))] * 2,
            *[dma((four, 8))] * 6,
            *[dma((2, 16))] * 4,
        ],
        compiler_params=pltpu.CompilerParams(
            collective_id=0, has_side_effects=True, vmem_limit_bytes=56 * 2**20),
    )(filtered, weights, probes)


def per_device(images, classes, ctf_table, weights, probes):
    onehot = (classes[:, None] == jnp.arange(ctf_table.shape[0])[None, :]).astype(jnp.bfloat16)
    filters = jnp.dot(onehot, ctf_table, preferred_element_type=jnp.float32)
    filtered = (images.astype(jnp.float32) * filters).astype(jnp.bfloat16)
    spread = jnp.broadcast_to(weights.reshape(-1, 8, 1), (weights.shape[0] // 8, 8, WIDTH))
    image_sum, grams = sweeps(filtered, spread, probes.astype(jnp.bfloat16))
    n = probes.shape[1]
    return finish(image_sum, grams.reshape(2, n, n))


def solution(mesh):
    return jax.shard_map(
        per_device,
        mesh=mesh,
        in_specs=(P("img", "pix"), P("img"), P(None, "pix"), P("img"), P("pix", None)),
        out_specs=(P("pix", None), P()),
        check_vma=False,
    )
```

time: 268 us -> 176 us (0.66)
  blocking collectives: 162 us -> 0 us
  Pallas kernels: 25.2 us -> 164 us
  waiting for transfers between devices: 39.9 us -> 0 us
  starting transfers between devices: 14.9 us -> 0 us
  matrix products: 17 us -> 6.03 us
    all_to_all x11 -> x0, blocking collectives: 162 us -> none  [the longest x5 74.6 us: sent_to_all(): lax.all_to_all(jnp.broadcast_to(x[None], (devices, *x.shape)), axis, 0, 0...]
    pallas_call x0 -> x1, Pallas kernels: none -> 139 us  [sweeps(): pl.pallas_call(sweeps_kernel, out_shape=(jax.ShapeDtypeStruct((n, pixels)...]
    all_to_all x3 -> x0, waiting for transfers between devices: 39.9 us -> none  [the longest x1 20.6 us: summed_on_arrival(): lax.all_to_all(blocks, axis, split_axis=0, concat_axis=0, tiled=True)]
    all_to_all x3 -> x0, starting transfers between devices: 14.9 us -> none  [the longest x1 7.58 us: summed_on_arrival(): lax.all_to_all(blocks, axis, split_axis=0, concat_axis=0, tiled=True)]
    dot_general x6 -> x0, matrix products: 12.7 us -> none  [the longest x2 8.05 us: power_step(): jnp.dot(filtered, probe_half, preferred_element_type=jnp.float32)]
  transfers between devices with their start and end apart: 3 -> 0, of which waited for: 3 -> 0; matrix products, arithmetic and copies ran while one was open for 1% -> 0% of each run, Pallas kernels for 0% -> 0%
where the time goes in v2:
time: 176 us
  Pallas kernels  164 us (93%)
  matrix products  6.03 us (3%)
  local copies, waits for them, and re-layouts  2.57 us (1%)
  other arithmetic  2.07 us (1%)
    pallas_call x1, Pallas kernels, sweeps(): pl.pallas_call(sweeps_kernel, out_shape=(jax.ShapeDtypeStruct((n, pixels)...  139 us
    pallas_call x1, Pallas kernels, finish(): pl.pallas_call(finish_kernel, out_shape=(jax.ShapeDtypeStruct((rows, n),...  24.9 us
    dot_general x1, matrix products, per_device(): filters = jnp.dot(onehot, ctf_table, preferred_element_type=jnp.float32)  6.03 us

profile of v2, /device:TPU:1, one launch (start us, length us, event | category | flops | bytes accessed | tf_op | source)
XLA Modules:
  0.0 175.7 jit_solution(10423699875584466183)
XLA Ops:
  0.6 0.0 copy-start
  0.6 0.9 broadcast_in_dim.4
  1.6 2.1 %convert_element_type.12.probes = bf16[1024,256]{1,0:T(8,128)(2,1)} convert(f32[1024,256]{1,0:T(8,128)} %param.9) | non-fusion elementwise | flops 262144 | bytes 1572864 | tf_op jit(solution)/shard_map/convert_element_type | solution.py:388
  3.6 1.7 broadcast_in_dim.10.weights
  5.3 0.0 copy-done
  5.3 6.0 %multiply_convert_fusion.filtered = bf16[3200,1024]{1,0:T(8,128)(2,1)} fusion(bf16[3200,1024]{1,0:T(8,128)(2,1)} %param.5, bf16[64,1024]{1,0:T(8,128)(2,1)S(1)} %copy-done, s32[3200]{0:T(1024)} %param.6), kind=kOutput, calls=%fused_computation | convolution fusion | flops 429465600 | bytes 13251072 | tf_op jit(solution)/shard_map/dot_general | solution.py:385
  11.3 139.4 %shard_map.68 = (bf16[256,1024]{1,0:T(8,128)(2,1)}, f32[2,16,16,256]{3,2,1,0:T(8,128)}) custom-call(bf16[3200,1024]{1,0:T(8,128)(2,1)} %multiply_convert_fusion.filtered, f32[400,8,128]{2,1,0:T(8,128)} %broadcast_in_dim.10.weights, bf16[1024,256]{1,0:T(8,128)(2,1)} %convert_element_type.12.probes), custom_call_target="tpu_custom_call" | custom-call | tf_op jit(solution)/shard_map/pallas_call | solution.py:355
  150.7 24.9 %shard_map.69 = (f32[1024,256]{1,0:T(8,128)}, f32[256,256]{1,0:T(8,128)}) custom-call(bf16[256,1024]{1,0:T(8,128)(2,1)} %get-tuple-element.4.image_sum, f32[2,256,256]{2,1,0:T(8,128)} %bitcast.2), custom_call_target="tpu_custom_call" | custom-call | tf_op jit(solution)/shard_map/pallas_call | solution.py:76
Async XLA Ops:
  0.6 4.7 %copy-start = (bf16[64,1024]{1,0:T(8,128)(2,1)S(1)}, bf16[64,1024]{1,0:T(8,128)(2,1)}, u32[]{:S(2)}) copy-start(bf16[64,1024]{1,0:T(8,128)(2,1)} %param.7) | copy-start | bytes 393220

commit v3 on v2

--- a/solution.py
+++ b/solution.py
@@ -13,6 +13,20 @@
 
 def product(a, b, dims=((1,), (0,))):
     return lax.dot_general(a, b, (dims, ((), ())), precision=HIGHEST, preferred_element_type=jnp.float32)
+
+
+def split(a):
+    top = a.astype(jnp.bfloat16)
+    return top, (a - top.astype(jnp.float32)).astype(jnp.bfloat16)
+
+
+def product3(a, b, dims=((1,), (0,))):
+    (a0, a1), (b0, b1) = split(a), split(b)
+
+    def one(p, q):
+        return lax.dot_general(p, q, (dims, ((), ())), preferred_element_type=jnp.float32)
+
+    return one(a0, b0) + (one(a0, b1) + one(a1, b0))
 
 
 def factor_blocks(gram, work, spread, small, inverse, upper):
@@ -49,7 +63,7 @@
             small[pl.ds(j, pair, stride=16), :] = row
         for g in range(pair):
             head = small[16 * g : 16 * g + 16, :]
-            lead = product(head, work[g, chunk : chunk + 128, :])
+            lead = product3(head, work[g, chunk : chunk + 128, :])
             wide = jnp.concatenate([head, head], axis=1) if n == 256 else head
             here = (col >= start) & (col < start + 16)
             mixed = jnp.where(here, wide, lead)
@@ -58,11 +72,11 @@
                 col >= start + lax.broadcasted_iota(jnp.int32, (16, n), 0), lead, 0.0)
             below = start + 16
             if below < n:
-                side = product(work[g, below:, chunk : chunk + 128], head, ((1,), (1,)))
+                side = product3(work[g, below:, chunk : chunk + 128], head, ((1,), (1,)))
                 cols = lax.broadcasted_iota(jnp.int32, (n - below, n), 1)
                 old = work[g, below:, :]
                 old = jnp.where((cols >= start) & (cols < below), 0.0, old)
-                work[g, below:, :] = old - product(side, mixed)
+                work[g, below:, :] = old - product3(side, mixed)
 
 
 def finish_kernel(image_sum, gram, basis, factor, work, spread, small, inverse, upper):
@@ -88,6 +102,7 @@
     )(image_sum, gram)
 
 
+FLIPS = ((1, 0), (0, 1), (1, 1))
 SHARE_TILES = ((7, 6, 6, 6), (6, 6, 7, 6))
 WIDTH = 128
 MESH = pl.DeviceIdType.MESH
@@ -103,15 +118,21 @@
         self.img, self.pix = lax.axis_index("img"), lax.axis_index("pix")
         self.z, self.core = self.img // 2, self.img % 2
         x, y = self.pix // 4, self.pix % 4
-        self.bits, self.across = [], []
+        self.x, self.y = x, y
+        self.bits = []
         for near, far in ((x, y), (y, x)):
             high, low = near // 2, near % 2
             self.bits.append(((high + low) % 2, high))
-        flips = ((x + 1 - 2 * (x % 2)) * 4 + y, (3 - x) * 4 + y, x * 4 + y + 1 - 2 * (y % 2), x * 4 + 3 - y)
         (xv, xu), (yv, yu) = self.bits
         self.bits = (xv, yv, xu, yu)
-        self.across = tuple((self.img, p) for p in (flips[0], flips[2], flips[1], flips[3]))
+        self.flipped = (x + 1 - 2 * (x % 2), y + 1 - 2 * (y % 2), 3 - x, 3 - y)
         self.partner = (self.z * 2 + 1 - self.core, self.pix)
+
+    def across(self, *links):
+        x, y = self.x, self.y
+        for k in links:
+            x, y = (x, self.flipped[k]) if k % 2 else (self.flipped[k], y)
+        return (self.img, x * 4 + y)
 
     def along_z(self, d):
         return ((self.z + d) % 8 * 2 + self.core, self.pix)
@@ -136,8 +157,9 @@
     return streams
 
 
-def sweep(here, sends, t, c, filtered, weights, probe, scores, landed, scaled, shares, crossed, halves, arrived, whole, sems):
-    rs_send, rs_recv, ag_send, ag_recv, d2d_send, d2d_recv, z_send, z_recv, g_send, g_recv, f_send, f_recv = sems
+def sweep(here, sends, t, c, prepare, filtered, weights, probe, scores, landed, scaled, shares, crossed, halves, arrived, whole, sems):
+    rs_send, rs_recv, ag_send, ag_recv, ws_send, ws_recv, wg_send, wg_recv = sems[:8]
+    d2d_send, d2d_recv, z_send, z_recv, g_send, g_recv, f_send, f_recv = sems[8:]
     streams = tiles_of(c)
     dims = ((1,), (0,)) if t == 0 else ((1,), (1,))
 
@@ -145,7 +167,7 @@
         return here.bits[(s + i) % 4]
 
     def across(s, i):
-        return here.across[(s + i) % 4]
+        return here.across((s + i) % 4)
 
     start = [[first] for first, _ in streams]
     flow = [[None] * 4 for _ in streams]
@@ -167,10 +189,13 @@
 
     slots = []
     at = 0
-    for i in range(4):
+    for i in range(2):
         for s in range(4):
             slots.append(at)
             at += streams[s][1] * 16 >> (i + 1)
+    for s in range(4):
+        slots.append(at)
+        at += 3 * streams[s][1]
 
     def send_half(s, i, give, half):
         flow[s][i] = remote(
@@ -179,15 +204,33 @@
         flow[s][i].start()
         sends.append(flow[s][i])
 
+    def piece(s, flip):
+        near, far = (1 - bit(s, i) if f else bit(s, i) for i, f in zip((2, 3), flip))
+        return pl.ds(start[s][2] + (2 * near + far) * streams[s][1], streams[s][1])
+
+    def to_three(s, send):
+        copies = []
+        for j, flip in enumerate(FLIPS):
+            links = [(s + i) % 4 for i, f in zip((2, 3), flip) if f]
+            copies.append(send(j, flip, here.across(*links)))
+            copies[-1].start()
+        sends.extend(copies)
+        return copies
+
+    def corner(s, j):
+        return pl.ds(slots[8 + s] + j * streams[s][1], streams[s][1])
+
     todo = []
     for s in range(4):
+        prepare(s)
         give, keep, half = pass_half(s, 0)
         score(give, half)
         send_half(s, 0, give, half)
         todo.append((keep, half))
     for keep, half in todo:
         score(keep, half)
-    for i in range(4):
+    wide = []
+    for i in range(2):
         yield ("rs", t, i)
         for s in range(4):
             half = streams[s][1] * 16 >> (i + 1)
@@ -195,13 +238,24 @@
             flow[s][i].wait_recv()
             mine = scores[pl.ds(keep, half)].astype(jnp.float32)
             mine = mine + landed[pl.ds(slots[4 * i + s], half)].astype(jnp.float32)
-            if i < 3:
-                scores[pl.ds(keep, half)] = mine.astype(jnp.bfloat16)
-                give, _, small = pass_half(s, i + 1)
-                send_half(s, i + 1, give, small)
+            scores[pl.ds(keep, half)] = mine.astype(jnp.bfloat16)
+            if i == 0:
+                give, _, small = pass_half(s, 1)
+                send_half(s, 1, give, small)
             else:
-                scaled[pl.ds(keep, half)] = (weights[pl.ds(keep, half)] * mine).astype(jnp.bfloat16)
-                flow[s][3] = None
+                wide.append(to_three(s, lambda j, flip, to: remote(
+                    scores.at[piece(s, flip)], landed.at[corner(s, j)], ws_send.at[j, s], ws_recv.at[j, s], to)))
+    yield ("rs", t, 2)
+    spread = []
+    for s in range(4):
+        own = piece(s, (0, 0))
+        mine = scores[own].astype(jnp.float32)
+        for j in range(3):
+            wide[s][j].wait_recv()
+            mine = mine + landed[corner(s, j)].astype(jnp.float32)
+        scaled[own] = (weights[own] * mine).astype(jnp.bfloat16)
+        spread.append(to_three(s, lambda j, flip, to: remote(
+            scaled.at[own], scaled.at[own], wg_send.at[j, s], wg_recv.at[j, s], to)))
     back = [[None] * 4 for _ in streams]
 
     def send_back(s, i):
@@ -211,14 +265,17 @@
         back[s][i].start()
         sends.append(back[s][i])
 
+    yield ("ag", t, 0)
     for s in range(4):
-        send_back(s, 3)
-    for i in (3, 2, 1, 0):
-        yield ("ag", t, 3 - i)
+        for copy in spread[s]:
+            copy.wait_recv()
+        send_back(s, 1)
+    for i in (1, 0):
+        yield ("ag", t, 2 - i)
         for s in range(4):
             back[s][i].wait_recv()
             if i:
-                send_back(s, i - 1)
+                send_back(s, 0)
     total = lax.dot_general(
         scaled[...].reshape(-1, WIDTH), filtered[...], (((0,), (0,)), ((), ())), preferred_element_type=jnp.float32)
     shares[...] = total.reshape(16, 8, -1).astype(jnp.bfloat16)
@@ -292,23 +349,50 @@
 
 
 def sweeps_kernel(
-    filtered, weights, probes, basis, grams,
-    scores, landed, scaled, shares, crossed, halves, arrived, whole, joined, parts, gram_landed, gram_whole,
-    rs_send, rs_recv, ag_send, ag_recv, d2d_send, d2d_recv, z_send, z_recv, g_send, g_recv, f_send, f_recv,
-    r_send, r_recv, a_send, a_recv,
+    images, classes, table, weights, probes, basis, grams,
+    filtered, row_weights, first_probe, scores, landed, scaled, shares, crossed, halves, arrived, whole, joined, parts, gram_landed, gram_whole,
+    rs_send, rs_recv, ag_send, ag_recv, ws_send, ws_recv, wg_send, wg_recv,
+    d2d_send, d2d_recv, z_send, z_recv, g_send, g_recv, f_send, f_recv,
+    r_send, r_recv, a_send, a_recv, load_sem,
 ):
     here = Place()
+    loads = []
+    for s, (first, share) in enumerate(tiles_of(0)):
+        rows = slice(first * 8, (first + 16 * share) * 8)
+        loads.append(pltpu.make_async_copy(images.at[rows], filtered.at[rows], load_sem.at[s]))
+        loads[-1].start()
+    first_probe[...] = probes[...].astype(jnp.bfloat16)
     greet(here)
     sends = []
-    all_sems = (rs_send, rs_recv, ag_send, ag_recv, d2d_send, d2d_recv, z_send, z_recv, g_send, g_recv, f_send, f_recv)
+    all_sems = (
+        rs_send, rs_recv, ag_send, ag_recv, ws_send, ws_recv, wg_send, wg_recv,
+        d2d_send, d2d_recv, z_send, z_recv, g_send, g_recv, f_send, f_recv)
+
+    def filter_block(b, _):
+        rows = pl.ds(pl.multiple_of(b * 128, 128), 128)
+        kinds = lax.broadcasted_iota(jnp.int32, (table.shape[0], 128), 0)
+        hot = jnp.where(kinds == classes[pl.ds(b, 1), :], 1.0, 0.0).astype(jnp.bfloat16)
+        filters = lax.dot_general(hot, table[...], (((0,), (0,)), ((), ())), preferred_element_type=jnp.float32)
+        filtered[rows, :] = (filtered[rows, :].astype(jnp.float32) * filters).astype(jnp.bfloat16)
+        return 0
+
+    def prepare(s):
+        first, share = tiles_of(0)[s]
+        loads[s].wait()
+        lax.fori_loop(first // 16, first // 16 + share, filter_block, 0)
+
+    def weigh_block(b, _):
+        column = jnp.broadcast_to(weights[pl.ds(b, 1), :], (128, 128)).T
+        row_weights[pl.ds(b * 16, 16)] = column.reshape(16, 8, 128)
+        return 0
 
     def run(c):
         cols = slice(c * WIDTH, (c + 1) * WIDTH)
         for t in range(ITERS):
-            probe = (lambda: probes[:, cols]) if t == 0 else (lambda: joined[0, cols, :])
+            probe = (lambda: first_probe[:, cols]) if t == 0 else (lambda: joined[0, cols, :])
             n = 2 * t + c
             yield from sweep(
-                here, sends, t, c, filtered, weights, probe, scores.at[n], landed.at[n], scaled.at[n], shares.at[n],
+                here, sends, t, c, prepare if n == 0 else lambda s: None, filtered, row_weights, probe, scores.at[n], landed.at[n], scaled.at[n], shares.at[n],
                 crossed.at[n], halves.at[n], arrived.at[n], whole.at[n], [sem.at[n] for sem in all_sems])
             found = whole[n].reshape(WIDTH, -1)
             if t == 0:
@@ -322,9 +406,9 @@
             here, sends, joined.at[0] if t == 0 else basis, gram_whole.at[t], parts.at[t], gram_landed.at[t], sems)
 
     live = [run(c) for c in range(2)]
-    label = next(live[0])
-    while label != LAG:
-        label = next(live[0])
+    for one in live:
+        next(one)
+    lax.fori_loop(0, weights.shape[0], weigh_block, 0)
     pending = True
     while live:
         for one in list(live):
@@ -341,11 +425,8 @@
         copy.wait_send()
 
 
-LAG = ("rs", 0, 0)
-
-
-def sweeps(filtered, weights, probes):
-    rows, pixels = filtered.shape
+def sweeps(images, classes, table, weights, probes):
+    rows, pixels = images.shape
     n = probes.shape[1]
     tiles = rows // 8
     four = 2 * ITERS
@@ -355,9 +436,12 @@
     return pl.pallas_call(
         sweeps_kernel,
         out_shape=(jax.ShapeDtypeStruct((n, pixels), bf16), jax.ShapeDtypeStruct((2, 16, 16, n), f32)),
-        in_specs=[vmem] * 3,
+        in_specs=[pl.BlockSpec(memory_space=pl.ANY)] + [vmem] * 4,
         out_specs=[vmem] * 2,
         scratch_shapes=[
+            pltpu.VMEM((rows, pixels), bf16),
+            pltpu.VMEM((tiles, 8, WIDTH), f32),
+            pltpu.VMEM((pixels, n), bf16),
             pltpu.VMEM((four, tiles, 8, WIDTH), bf16),
             pltpu.VMEM((four, tiles * 15 // 16, 8, WIDTH), bf16),
             pltpu.VMEM((four, tiles, 8, WIDTH), bf16),
@@ -370,22 +454,20 @@
             pltpu.VMEM((2, 16, 16, n), f32),
             pltpu.VMEM((2, 16, 16, n), f32),
             pltpu.VMEM((2, 16, 16, n), f32),
-            *[dma((four, 4, 4))] * 4,
+            *[dma((four, 2, 4))] * 4,
+            *[dma((four, 3, 4))] * 4,
             *[dma((four, 1))] * 2,
             *[dma((four, 8))] * 6,
             *[dma((2, 16))] * 4,
+            dma((4,)),
         ],
         compiler_params=pltpu.CompilerParams(
             collective_id=0, has_side_effects=True, vmem_limit_bytes=56 * 2**20),
-    )(filtered, weights, probes)
+    )(images, classes, table, weights, probes)
 
 
 def per_device(images, classes, ctf_table, weights, probes):
-    onehot = (classes[:, None] == jnp.arange(ctf_table.shape[0])[None, :]).astype(jnp.bfloat16)
-    filters = jnp.dot(onehot, ctf_table, preferred_element_type=jnp.float32)
-    filtered = (images.astype(jnp.float32) * filters).astype(jnp.bfloat16)
-    spread = jnp.broadcast_to(weights.reshape(-1, 8, 1), (weights.shape[0] // 8, 8, WIDTH))
-    image_sum, grams = sweeps(filtered, spread, probes.astype(jnp.bfloat16))
+    image_sum, grams = sweeps(images, classes.reshape(-1, 128), ctf_table, weights.reshape(-1, 128), probes)
     n = probes.shape[1]
     return finish(image_sum, grams.reshape(2, n, n))
 

time: 176 us -> 154 us (0.88)
  Pallas kernels: 164 us -> 154 us
  matrix products: 6.03 us -> 0 us
  local copies, waits for them, and re-layouts: 2.57 us -> 0 us
  other arithmetic: 2.07 us -> 0 us
    pallas_call x1, Pallas kernels: 139 us -> 133 us  [sweeps(): pl.pallas_call(sweeps_kernel, out_shape=(jax.ShapeDtypeStruct((n, pixels)...]
    dot_general x1 -> x0, matrix products: 6.03 us -> none  [per_device(): filters = jnp.dot(onehot, ctf_table, preferred_element_type=jnp.float32)]
    pallas_call x1, Pallas kernels: 24.9 us -> 20.9 us  [finish(): pl.pallas_call(finish_kernel, out_shape=(jax.ShapeDtypeStruct((rows, n),...]
    broadcast_in_dim x2 -> x0, local copies, waits for them, and re-layouts: 2.56 us -> none  [per_device(): jnp.broadcast_to(weights.reshape(-1, 8, 1), (weights.shape[0] // 8, 8, WI...]
    convert_element_type x1 -> x0, other arithmetic: 2.07 us -> none  [per_device(): image_sum, grams = sweeps(filtered, spread, probes.astype(jnp.bfloat16))]
where the time goes in v3:
time: 154 us
  Pallas kernels  154 us (100%)
    pallas_call x1, Pallas kernels, sweeps(): pl.pallas_call(sweeps_kernel, out_shape=(jax.ShapeDtypeStruct((n, pixels)...  133 us
    pallas_call x1, Pallas kernels, finish(): pl.pallas_call(finish_kernel, out_shape=(jax.ShapeDtypeStruct((rows, n),...  20.9 us

profile of v3, /device:TPU:1, one launch (start us, length us, event | category | flops | bytes accessed | tf_op | source)
XLA Modules:
  0.0 154.3 jit_solution(13398203845914628519)
XLA Ops:
  0.6 132.8 %shard_map.68 = (bf16[256,1024]{1,0:T(8,128)(2,1)}, f32[2,16,16,256]{3,2,1,0:T(8,128)}) custom-call(bf16[3200,1024]{1,0:T(8,128)(2,1)} %images.1, s32[25,128]{1,0:T(8,128)} %bitcast.4, bf16[64,1024]{1,0:T(8,128)(2,1)} %table.1, f32[25,128]{1,0:T(8,128)} %bitcast.5, f32[1024,256]{1,0:T(8,128)} %probes.1), custom_call_target="tpu_custom_call" | custom-call | tf_op jit(solution)/shard_map/pallas_call | solution.py:436
  133.4 20.9 %shard_map.69 = (f32[1024,256]{1,0:T(8,128)}, f32[256,256]{1,0:T(8,128)}) custom-call(bf16[256,1024]{1,0:T(8,128)(2,1)} %get-tuple-element.4.image_sum, f32[2,256,256]{2,1,0:T(8,128)} %bitcast.3), custom_call_target="tpu_custom_call" | custom-call | tf_op jit(solution)/shard_map/pallas_call | solution.py:90

commit v4 on v3

--- a/solution.py
+++ b/solution.py
@@ -81,8 +81,10 @@
 
 def finish_kernel(image_sum, gram, basis, factor, work, spread, small, inverse, upper):
     factor_blocks(gram, work, spread, small, inverse, upper)
-    basis[...] = product(inverse[1], image_sum[...].astype(jnp.float32)).T
-    factor[...] = product(inverse[0], upper[1], ((1,), (1,)))
+    flat = [lax.dot_general(p, image_sum[...], (((1,), (0,)), ((), ())), preferred_element_type=jnp.float32)
+            for p in split(inverse[1])]
+    basis[...] = (flat[0] + flat[1]).T
+    factor[...] = product3(inverse[0], upper[1], ((1,), (1,)))
 
 
 def finish(image_sum, gram):
@@ -102,7 +104,9 @@
     )(image_sum, gram)
 
 
-FLIPS = ((1, 0), (0, 1), (1, 1))
+FLIPS = ((1, 1), (1, 0), (0, 1))
+FAR_Z = (4, 3, 5, 2, 6, 1, 7)
+FAR_PLANE = tuple(sorted(range(1, 16), key=lambda d: -(min(d // 4, 4 - d // 4) + min(d % 4, 4 - d % 4))))
 SHARE_TILES = ((7, 6, 6, 6), (6, 6, 7, 6))
 WIDTH = 128
 MESH = pl.DeviceIdType.MESH
@@ -138,7 +142,7 @@
         return ((self.z + d) % 8 * 2 + self.core, self.pix)
 
     def in_plane(self, d):
-        return (self.img, (self.pix + d) % 16)
+        return (self.img, (self.x + d // 4) % 4 * 4 + (self.y + d % 4) % 4)
 
 
 def greet(here):
@@ -146,7 +150,7 @@
     peers = [here.in_plane(d) for d in range(1, 16)] + [here.along_z(d) for d in range(1, 8)] + [here.partner]
     for peer in peers:
         pl.semaphore_signal(barrier, inc=1, device_id=peer, device_id_type=MESH)
-    pl.semaphore_wait(barrier, len(peers))
+    return lambda: pl.semaphore_wait(barrier, len(peers))
 
 
 def tiles_of(c):
@@ -157,7 +161,7 @@
     return streams
 
 
-def sweep(here, sends, t, c, prepare, filtered, weights, probe, scores, landed, scaled, shares, crossed, halves, arrived, whole, sems):
+def sweep(here, sends, t, c, prepare, ready, filtered, weights, probe, scores, landed, scaled, shares, crossed, halves, arrived, whole, sems):
     rs_send, rs_recv, ag_send, ag_recv, ws_send, ws_recv, wg_send, wg_recv = sems[:8]
     d2d_send, d2d_recv, z_send, z_recv, g_send, g_recv, f_send, f_recv = sems[8:]
     streams = tiles_of(c)
@@ -225,8 +229,11 @@
         prepare(s)
         give, keep, half = pass_half(s, 0)
         score(give, half)
+        if s == 0:
+            ready()
         send_half(s, 0, give, half)
         todo.append((keep, half))
+    yield ("keep", t, 0)
     for keep, half in todo:
         score(keep, half)
     wide = []
@@ -284,33 +291,33 @@
     sends.append(swap)
     yield ("img", t, 0)
     swap.wait_recv()
-    rounds = []
-    for d in range(1, 8):
+    rounds = {}
+    for d in FAR_Z:
         k = (here.z + d) % 8
         pair = shares[here.core * 8 + k].astype(jnp.float32) + crossed[k].astype(jnp.float32)
         halves[d] = pair.astype(jnp.bfloat16)
         copy = remote(halves.at[d], arrived.at[d], z_send.at[d], z_recv.at[d], here.along_z(d))
         copy.start()
-        rounds.append(copy)
-    sends.extend(rounds)
+        rounds[d] = copy
+    sends.extend(rounds.values())
     own = shares[here.core * 8 + here.z].astype(jnp.float32) + crossed[here.z].astype(jnp.float32)
     yield ("img", t, 1)
-    for d, copy in enumerate(rounds, 1):
-        copy.wait_recv()
+    for d in FAR_Z[::-1]:
+        rounds[d].wait_recv()
         own = own + arrived[d].astype(jnp.float32)
     mine = here.core * 8 + here.z
     whole[mine] = own.astype(jnp.bfloat16)
-    rounds = []
-    for d in range(1, 8):
+    rounds = {}
+    for d in FAR_Z:
         copy = remote(whole.at[mine], whole.at[mine], g_send.at[d], g_recv.at[d], here.along_z(d))
         copy.start()
-        rounds.append(copy)
-    sends.extend(rounds)
+        rounds[d] = copy
+    sends.extend(rounds.values())
     over = [remote(whole.at[mine], whole.at[mine], f_send.at[0], f_recv.at[0], here.partner)]
     over[0].start()
     yield ("img", t, 2)
-    for d, copy in enumerate(rounds, 1):
-        copy.wait_recv()
+    for d in FAR_Z[::-1]:
+        rounds[d].wait_recv()
         k = here.core * 8 + (here.z + 8 - d) % 8
         fwd = remote(whole.at[k], whole.at[k], f_send.at[d], f_recv.at[d], here.partner)
         fwd.start()
@@ -326,19 +333,19 @@
     gram = lax.dot_general(basis[...], basis[...], (((1,), (1,)), ((), ())), preferred_element_type=jnp.float32)
     parts[...] = gram.reshape(16, 16, -1)
     rounds = []
-    for d in range(1, 16):
-        copy = remote(parts.at[(here.pix + d) % 16], landed.at[d], r_send.at[d], r_recv.at[d], here.in_plane(d))
+    for d in FAR_PLANE:
+        copy = remote(parts.at[here.in_plane(d)[1]], landed.at[d], r_send.at[d], r_recv.at[d], here.in_plane(d))
         copy.start()
         rounds.append(copy)
     sends.extend(rounds)
     own = parts[here.pix]
     yield ("gram", 0, 0)
-    for d, copy in enumerate(rounds, 1):
+    for d, copy in zip(FAR_PLANE[::-1], rounds[::-1]):
         copy.wait_recv()
         own = own + landed[d]
     out[here.pix] = own
     rounds = []
-    for d in range(1, 16):
+    for d in FAR_PLANE:
         copy = remote(out.at[here.pix], out.at[here.pix], a_send.at[d], a_recv.at[d], here.in_plane(d))
         copy.start()
         rounds.append(copy)
@@ -362,7 +369,7 @@
         loads.append(pltpu.make_async_copy(images.at[rows], filtered.at[rows], load_sem.at[s]))
         loads[-1].start()
     first_probe[...] = probes[...].astype(jnp.bfloat16)
-    greet(here)
+    all_here = greet(here)
     sends = []
     all_sems = (
         rs_send, rs_recv, ag_send, ag_recv, ws_send, ws_recv, wg_send, wg_recv,
@@ -392,7 +399,7 @@
             probe = (lambda: first_probe[:, cols]) if t == 0 else (lambda: joined[0, cols, :])
             n = 2 * t + c
             yield from sweep(
-                here, sends, t, c, prepare if n == 0 else lambda s: None, filtered, row_weights, probe, scores.at[n], landed.at[n], scaled.at[n], shares.at[n],
+                here, sends, t, c, *((prepare, all_here) if n == 0 else (lambda s: None, lambda: None)), filtered, row_weights, probe, scores.at[n], landed.at[n], scaled.at[n], shares.at[n],
                 crossed.at[n], halves.at[n], arrived.at[n], whole.at[n], [sem.at[n] for sem in all_sems])
             found = whole[n].reshape(WIDTH, -1)
             if t == 0:
@@ -406,7 +413,7 @@
             here, sends, joined.at[0] if t == 0 else basis, gram_whole.at[t], parts.at[t], gram_landed.at[t], sems)
 
     live = [run(c) for c in range(2)]
-    for one in live:
+    for one in live + live:
         next(one)
     lax.fori_loop(0, weights.shape[0], weigh_block, 0)
     pending = True

time: 154 us -> 146 us (0.948)
  Pallas kernels: 154 us -> 145 us
    pallas_call x1, Pallas kernels: 133 us -> 125 us  [sweeps(): pl.pallas_call(sweeps_kernel, out_shape=(jax.ShapeDtypeStruct((n, pixels)...]
where the time goes in v4:
time: 146 us
  Pallas kernels  145 us (99%)
    pallas_call x1, Pallas kernels, sweeps(): pl.pallas_call(sweeps_kernel, out_shape=(jax.ShapeDtypeStruct((n, pixels)...  125 us
    pallas_call x1, Pallas kernels, finish(): pl.pallas_call(finish_kernel, out_shape=(jax.ShapeDtypeStruct((rows, n),...  20.3 us

profile of v4, /device:TPU:1, one launch (start us, length us, event | category | flops | bytes accessed | tf_op | source)
XLA Modules:
  0.0 146.0 jit_solution(2694660918477538207)
XLA Ops:
  0.6 125.1 %shard_map.68 = (bf16[256,1024]{1,0:T(8,128)(2,1)}, f32[2,16,16,256]{3,2,1,0:T(8,128)}) custom-call(bf16[3200,1024]{1,0:T(8,128)(2,1)} %images.1, s32[25,128]{1,0:T(8,128)} %bitcast.4, bf16[64,1024]{1,0:T(8,128)(2,1)} %table.1, f32[25,128]{1,0:T(8,128)} %bitcast.5, f32[1024,256]{1,0:T(8,128)} %probes.1), custom_call_target="tpu_custom_call" | custom-call | tf_op jit(solution)/shard_map/pallas_call | solution.py:443
  125.7 20.3 %shard_map.69 = (f32[1024,256]{1,0:T(8,128)}, f32[256,256]{1,0:T(8,128)}) custom-call(bf16[256,1024]{1,0:T(8,128)(2,1)} %get-tuple-element.4.image_sum, f32[2,256,256]{2,1,0:T(8,128)} %bitcast.3), custom_call_target="tpu_custom_call" | custom-call | tf_op jit(solution)/shard_map/pallas_call | solution.py:92

commit v5 on v4

--- a/solution.py
+++ b/solution.py
@@ -7,13 +7,7 @@
 
 ITERS = 2
 
-HIGHEST = lax.Precision.HIGHEST
-UP = float(2.0**24)
 DOWN = float(2.0**-24)
-
-def product(a, b, dims=((1,), (0,))):
-    return lax.dot_general(a, b, (dims, ((), ())), precision=HIGHEST, preferred_element_type=jnp.float32)
-
 
 def split(a):
     top = a.astype(jnp.bfloat16)
@@ -41,17 +35,17 @@
             block = work[g, start : start + 16, chunk : chunk + 128]
             for j in range(16):
                 spread[j, 16 * g : 16 * g + 16, :] = jnp.broadcast_to(block[:, off + j : off + j + 1], (16, 128))
-        a = {(i, j): spread[j, pl.ds(i, pair, stride=16), :] for j in range(16) for i in range(j, 16)}
-        inv = []
+        a = {}
         t = {}
         for j in range(16):
-            root = lax.rsqrt(a[j, j])
-            inv.append(root)
-            for i in range(j + 1, 16):
-                a[i, j] = a[i, j] * root
-            for m in range(j + 1, 16):
-                for i in range(m, 16):
-                    a[i, m] = a[i, m] - a[i, j] * a[m, j]
+            for i in range(j, 16):
+                entry = spread[j, pl.ds(i, pair, stride=16), :]
+                for q in range(j):
+                    entry = entry - a[i, q] * a[j, q]
+                if i == j:
+                    root = lax.rsqrt(entry)
+                else:
+                    a[i, j] = entry * root
             t[j, j] = root
             row = jnp.where(lane == off + j, root, 0.0)
             for m in range(j):
@@ -363,13 +357,13 @@
     r_send, r_recv, a_send, a_recv, load_sem,
 ):
     here = Place()
+    all_here = greet(here)
     loads = []
     for s, (first, share) in enumerate(tiles_of(0)):
         rows = slice(first * 8, (first + 16 * share) * 8)
         loads.append(pltpu.make_async_copy(images.at[rows], filtered.at[rows], load_sem.at[s]))
         loads[-1].start()
     first_probe[...] = probes[...].astype(jnp.bfloat16)
-    all_here = greet(here)
     sends = []
     all_sems = (
         rs_send, rs_recv, ag_send, ag_recv, ws_send, ws_recv, wg_send, wg_recv,

time: 146 us -> 146 us (level)
  no operation moved by 1% of the time
where the time goes in v5:
time: 146 us; the launch traced here: 145 us
  Pallas kernels  145 us (99%)
    pallas_call x1, Pallas kernels, sweeps(): pl.pallas_call(sweeps_kernel, out_shape=(jax.ShapeDtypeStruct((n, pixels)...  125 us
    pallas_call x1, Pallas kernels, finish(): pl.pallas_call(finish_kernel, out_shape=(jax.ShapeDtypeStruct((rows, n),...  19.8 us

profile of v5, /device:TPU:1, one launch (start us, length us, event | category | flops | bytes accessed | tf_op | source)
XLA Modules:
  0.0 145.4 jit_solution(5923309432172585593)
XLA Ops:
  0.6 124.9 %shard_map.68 = (bf16[256,1024]{1,0:T(8,128)(2,1)}, f32[2,16,16,256]{3,2,1,0:T(8,128)}) custom-call(bf16[3200,1024]{1,0:T(8,128)(2,1)} %images.1, s32[25,128]{1,0:T(8,128)} %bitcast.4, bf16[64,1024]{1,0:T(8,128)(2,1)} %table.1, f32[25,128]{1,0:T(8,128)} %bitcast.5, f32[1024,256]{1,0:T(8,128)} %probes.1), custom_call_target="tpu_custom_call" | custom-call | tf_op jit(solution)/shard_map/pallas_call | solution.py:437
  125.5 19.8 %shard_map.69 = (f32[1024,256]{1,0:T(8,128)}, f32[256,256]{1,0:T(8,128)}) custom-call(bf16[256,1024]{1,0:T(8,128)(2,1)} %get-tuple-element.4.image_sum, f32[2,256,256]{2,1,0:T(8,128)} %bitcast.3), custom_call_target="tpu_custom_call" | custom-call | tf_op jit(solution)/shard_map/pallas_call | solution.py:86
